TPU v7x, 128 devices: a whole 4x4x4 slice. The times are simulated.
128 devices in a mesh: gx: 8 (over x, core), gy: 16 (over y, z).
Axes of the slice: x: 4, y: 4, z: 4, core: 2. Of those that a mesh axis runs over, the one named last changes fastest.
Arguments:
- electric: float32 [3, 128, 256, 256], P(None, 'gx', 'gy'), may hold values from -6 to 6
- magnetic: float32 [3, 128, 256, 256], P(None, 'gx', 'gy'), may hold values from -6 to 6
- aux_electric: float32 [6, 128, 256, 256], P(None, 'gx', 'gy'), may hold values from -3 to 3
- aux_magnetic: float32 [6, 128, 256, 256], P(None, 'gx', 'gy'), may hold values from -3 to 3
- grades: int32 [3, 128, 256, 256], P(None, 'gx', 'gy'), may hold values from 0 to 3
- permittivity: float32 [128, 256, 256], P('gx', 'gy'), may hold values from 1 to 8
- dipole_cell: int32 [3, 65536], P(None, ('gx', 'gy')), may hold values from 0 to 255, as said below
- dipole_port: int32 [65536], P(('gx', 'gy')), may hold values from 0 to 511
- live_count: int32 [128], P(('gx', 'gy')), may hold values from 1 to 512, as said below
- injection: bfloat16 [65536, 512], P(('gx', 'gy')), may hold values from -0.25 to 0.25
- waveform: bfloat16 [512, 16], replicated, may hold values from -6 to 6
Outputs:
- electric_out: float32 [3, 128, 256, 256], P(None, 'gx', 'gy')
- magnetic_out: float32 [3, 128, 256, 256], P(None, 'gx', 'gy')
- port_power: float32 [16, 512], replicated
Inputs may be any that keep to these rules, and one draw needn't show every extreme that they name: `dipole_cell`: slot s lies in the block of cells held by the device that holds slot s. The live slots of a device are its first live_count ones; some device has all 512 live.
All inputs are finite; a program needn't handle non-finite values.
Results may differ from a plain program's by a relative error of at most 0.0003.
Values sent between devices are 32-bit elements; how exact they have to be, the bound alone decides.
A program may use at most 128 MiB of HBM per device.

v0:
```python
import functools

import jax
import jax.numpy as jnp
from jax import lax
from jax.sharding import Mesh
from jax.sharding import PartitionSpec as P

GX = ("gx_0", "gx_1")
GY = ("gy_0", "gy_1")
GX_GY = ("gx_0", "gx_1", "gy_0", "gy_1")


courant = 0.55
absorb_keep = (0.0, 0.92, 0.75, 0.45)
absorb_take = (0.0, -0.06, -0.18, -0.35)
derivative_pairs = ((2, 1), (1, 2), (0, 2), (2, 0), (1, 0), (0, 1))


def passed_along(block, axis, distance):
    devices = range(lax.axis_size(axis))
    route = [(i - distance, i) for i in devices if i - distance in devices]
    return lax.ppermute(block, axis, route)


def over_axes(value, axes):
    return functools.reduce(lax.psum, axes, value)


def difference(values, axis, plane, forward):
    length = values.shape[axis]
    if plane is None:
        shape = list(values.shape)
        shape[axis] = 1
        plane = jnp.zeros(shape, values.dtype)
    if forward:
        after = jnp.concatenate([lax.slice_in_dim(values, 1, length, axis=axis), plane], axis)
        return after - values
    before = jnp.concatenate([plane, lax.slice_in_dim(values, 0, length - 1, axis=axis)], axis)
    return values - before


def grade_table(grades, table):
    result = jnp.zeros(grades.shape, jnp.float32)
    for level in range(1, 4):
        result = result + jnp.where(grades == level, table[level], 0.0)
    return result


def curl_parts(field, auxiliary, keep, take, planes, forward):
    terms = []
    updated = []
    for number, (component, axis) in enumerate(derivative_pairs):
        plane = None
        if planes is not None and axis == 0:
            plane = planes[0][component - 1]
        if planes is not None and axis == 1:
            plane = planes[1][component // 2]
        slope = difference(field[component], axis, plane, forward)
        carried = keep[axis] * auxiliary[number] + take[axis] * slope
        terms.append(slope + carried)
        updated.append(carried)
    rotation = (terms[0] - terms[1], terms[2] - terms[3], terms[4] - terms[5])
    return (rotation, tuple(updated))


def inject(z_plane, current_now, cell_table, depth_table):
    weighted = cell_table * current_now[:, None]
    source = lax.dot_general(
        weighted, depth_table, (((0,), (0,)), ((), ())), precision=lax.Precision.HIGHEST
    )
    return z_plane - courant * source.reshape(z_plane.shape)


def read_cells(z_plane, cell_table, depth_table):
    rows = z_plane.reshape(cell_table.shape[1], depth_table.shape[1])
    picked = jnp.dot(cell_table, rows, precision=lax.Precision.HIGHEST)
    return jnp.sum(picked * depth_table, axis=1)


def note_power(record, drive, index):
    return lax.dynamic_update_slice_in_dim(record, drive[None, :], index, 0)


def local(
    electric,
    magnetic,
    aux_electric,
    aux_magnetic,
    grades,
    permittivity,
    dipole_cell,
    dipole_port,
    live_count,
    injection,
    waveform,
):
    depth_x, depth_y, depth_z = electric.shape[1:]
    slots = dipole_cell.shape[1]
    ports, steps = waveform.shape
    row_index = lax.axis_index(GX)
    col_index = lax.axis_index(GY)
    plane_cell = (dipole_cell[0] - row_index * depth_x) * depth_y + (
        dipole_cell[1] - col_index * depth_y
    )
    cell_table = (
        plane_cell[:, None] == jnp.arange(depth_x * depth_y, dtype=jnp.int32)[None, :]
    ).astype(jnp.float32)
    depth_table = (dipole_cell[2][:, None] == jnp.arange(depth_z, dtype=jnp.int32)[None, :]).astype(
        jnp.float32
    )
    live = (jnp.arange(slots, dtype=jnp.int32) < live_count[0]).astype(jnp.float32)
    current = jnp.dot(injection, waveform, preferred_element_type=jnp.float32) * live[:, None]
    members = (dipole_port[:, None] == jnp.arange(ports, dtype=jnp.int32)[None, :]).astype(
        jnp.float32
    )
    factor = courant / permittivity
    keep = grade_table(grades, absorb_keep)
    take = grade_table(grades, absorb_take)
    record = jnp.zeros((steps, slots), jnp.float32)

    def turn_parts(step, carry):
        field_e, field_h, memory_e, memory_h, record = carry
        next_x = passed_along(jnp.stack([field_e[1][0:1], field_e[2][0:1]]), GX, -1)
        next_y = passed_along(jnp.stack([field_e[0][:, 0:1], field_e[2][:, 0:1]]), GY, -1)
        rotation, memory_e = curl_parts(field_e, memory_e, keep, take, (next_x, next_y), True)
        field_h = tuple((field_h[number] - courant * rotation[number] for number in range(3)))
        prior_x = passed_along(jnp.stack([field_h[1][-1:], field_h[2][-1:]]), GX, 1)
        prior_y = passed_along(jnp.stack([field_h[0][:, -1:], field_h[2][:, -1:]]), GY, 1)
        rotation, memory_h = curl_parts(field_h, memory_h, keep, take, (prior_x, prior_y), False)
        current_now = lax.dynamic_slice_in_dim(current, step, 1, 1)[:, 0]
        z_plane = inject(field_e[2] + factor * rotation[2], current_now, cell_table, depth_table)
        field_e = (field_e[0] + factor * rotation[0], field_e[1] + factor * rotation[1], z_plane)
        drive = current_now * read_cells(z_plane, cell_table, depth_table)
        record = note_power(record, drive, step)
        return (field_e, field_h, memory_e, memory_h, record)

    start_state = (
        tuple((electric[number] for number in range(3))),
        tuple((magnetic[number] for number in range(3))),
        tuple((aux_electric[number] for number in range(6))),
        tuple((aux_magnetic[number] for number in range(6))),
        record,
    )
    parts_e, parts_h, parts_me, parts_mh, record = lax.fori_loop(0, steps, turn_parts, start_state)
    electric = jnp.stack(parts_e)
    magnetic = jnp.stack(parts_h)
    partial_value = jnp.dot(record, members, precision=lax.Precision.HIGHEST)
    port_power = over_axes(partial_value, GX_GY)
    return (electric, magnetic, port_power)


def solution(mesh):
    split = Mesh(mesh.devices.reshape(4, 2, 4, 4), ("gx_0", "gx_1", "gy_0", "gy_1"))
    return jax.shard_map(
        local,
        mesh=split,
        in_specs=(
            P(None, GX, GY, None),
            P(None, GX, GY, None),
            P(None, GX, GY, None),
            P(None, GX, GY, None),
            P(None, GX, GY, None),
            P(GX, GY, None),
            P(None, GX_GY),
            P(GX_GY),
            P(GX_GY),
            P(GX_GY, None),
            P(),
        ),
        out_specs=(P(None, GX, GY, None), P(None, GX, GY, None), P()),
        check_vma=False,
    )
```

profile of v0, /device:TPU:1, one launch (start us, length us, event | category | flops | bytes accessed | tf_op | source)
XLA Modules:
  0.0 631.0 jit_solution(17114539362646406241)
XLA Ops:
  10.6 561.5 %while.50 = (s32[]{:T(128)}, f32[16,16,256]{2,1,0:T(8,128)S(1)}, f32[16,16,256]{2,1,0:T(8,128)S(1)}, f32[16,16,256]{2,1,0:T(8,128)S(1)}, f32[16,16,256]{2,1,0:T(...) while((s32[]{:T(128)}, f32[16,16,256]{2,1,0:T(8,128)S(1)}, ...), condition=%wide.region_2.3_spmd.clone, body=%wide.region_0.2_spmd.clone.sunk | while | flops 812285952 | bytes 56044672 | solution.py:145
  12.0 3.3 collective-permute-start
  22.5 2.4 multiply_subtract_fusion.7
  25.5 4.3 collective-permute-start.2
  31.7 3.4 collective-permute-start.3
  57.8 4.2 collective-permute-start.2
  63.9 4.6 collective-permute-start.3
  88.2 2.4 multiply_subtract_fusion.7
  91.2 4.2 collective-permute-start.2
  97.3 4.6 collective-permute-start.3
  121.6 2.4 multiply_subtract_fusion.7
  124.6 5.8 collective-permute-start.2
  132.3 4.5 collective-permute-start.3
  156.6 2.4 multiply_subtract_fusion.7
  159.6 6.4 %collective-permute-start.2 = (f32[2,16,1,256]{3,2,1,0:T(1,128)S(1)}, f32[2,16,1,256]{3,2,1,0:T(1,128)S(1)}, u32[]{:S(2)}, u32[]{:S(2)}) collective-permute-start(f32[2,16,1,256]{3,2,1,0:T(1,128)S(1)} %pad_maximum_fusion.12), channel_id=1, source_target_pairs={{0,1},{1,2},{2,3},{3,4},{4,5},{5,6},{6,7},{7,8},{8,9},{9,10},{10,1... | collective-permute-start | bytes 98312 | tf_op jit(solution)/shard_map/while/body/eval_jaxpr/ppermute | solution.py:23
  167.8 4.5 collective-permute-start.3
  195.1 6.4 %collective-permute-start.2 = (f32[2,16,1,256]{3,2,1,0:T(1,128)S(1)}, f32[2,16,1,256]{3,2,1,0:T(1,128)S(1)}, u32[]{:S(2)}, u32[]{:S(2)}) collective-permute-start(f32[2,16,1,256]{3,2,1,0:T(1,128)S(1)} %pad_maximum_fusion.12), channel_id=1, source_target_pairs={{0,1},{1,2},{2,3},{3,4},{4,5},{5,6},{6,7},{7,8},{8,9},{9,10},{10,1... | collective-permute-start | bytes 98312 | tf_op jit(solution)/shard_map/while/body/eval_jaxpr/ppermute | solution.py:23
  203.3 4.5 collective-permute-start.3
  230.6 6.4 %collective-permute-start.2 = (f32[2,16,1,256]{3,2,1,0:T(1,128)S(1)}, f32[2,16,1,256]{3,2,1,0:T(1,128)S(1)}, u32[]{:S(2)}, u32[]{:S(2)}) collective-permute-start(f32[2,16,1,256]{3,2,1,0:T(1,128)S(1)} %pad_maximum_fusion.12), channel_id=1, source_target_pairs={{0,1},{1,2},{2,3},{3,4},{4,5},{5,6},{6,7},{7,8},{8,9},{9,10},{10,1... | collective-permute-start | bytes 98312 | tf_op jit(solution)/shard_map/while/body/eval_jaxpr/ppermute | solution.py:23
  238.8 4.5 collective-permute-start.3
  266.1 6.4 %collective-permute-start.2 = (f32[2,16,1,256]{3,2,1,0:T(1,128)S(1)}, f32[2,16,1,256]{3,2,1,0:T(1,128)S(1)}, u32[]{:S(2)}, u32[]{:S(2)}) collective-permute-start(f32[2,16,1,256]{3,2,1,0:T(1,128)S(1)} %pad_maximum_fusion.12), channel_id=1, source_target_pairs={{0,1},{1,2},{2,3},{3,4},{4,5},{5,6},{6,7},{7,8},{8,9},{9,10},{10,1... | collective-permute-start | bytes 98312 | tf_op jit(solution)/shard_map/while/body/eval_jaxpr/ppermute | solution.py:23
  274.3 4.5 collective-permute-start.3
  301.6 6.4 %collective-permute-start.2 = (f32[2,16,1,256]{3,2,1,0:T(1,128)S(1)}, f32[2,16,1,256]{3,2,1,0:T(1,128)S(1)}, u32[]{:S(2)}, u32[]{:S(2)}) collective-permute-start(f32[2,16,1,256]{3,2,1,0:T(1,128)S(1)} %pad_maximum_fusion.12), channel_id=1, source_target_pairs={{0,1},{1,2},{2,3},{3,4},{4,5},{5,6},{6,7},{7,8},{8,9},{9,10},{10,1... | collective-permute-start | bytes 98312 | tf_op jit(solution)/shard_map/while/body/eval_jaxpr/ppermute | solution.py:23
  309.8 4.5 collective-permute-start.3
  334.1 2.4 multiply_subtract_fusion.7
  337.1 6.4 %collective-permute-start.2 = (f32[2,16,1,256]{3,2,1,0:T(1,128)S(1)}, f32[2,16,1,256]{3,2,1,0:T(1,128)S(1)}, u32[]{:S(2)}, u32[]{:S(2)}) collective-permute-start(f32[2,16,1,256]{3,2,1,0:T(1,128)S(1)} %pad_maximum_fusion.12), channel_id=1, source_target_pairs={{0,1},{1,2},{2,3},{3,4},{4,5},{5,6},{6,7},{7,8},{8,9},{9,10},{10,1... | collective-permute-start | bytes 98312 | tf_op jit(solution)/shard_map/while/body/eval_jaxpr/ppermute | solution.py:23
  345.4 4.5 collective-permute-start.3
  369.6 2.4 multiply_subtract_fusion.7
  372.6 6.4 %collective-permute-start.2 = (f32[2,16,1,256]{3,2,1,0:T(1,128)S(1)}, f32[2,16,1,256]{3,2,1,0:T(1,128)S(1)}, u32[]{:S(2)}, u32[]{:S(2)}) collective-permute-start(f32[2,16,1,256]{3,2,1,0:T(1,128)S(1)} %pad_maximum_fusion.12), channel_id=1, source_target_pairs={{0,1},{1,2},{2,3},{3,4},{4,5},{5,6},{6,7},{7,8},{8,9},{9,10},{10,1... | collective-permute-start | bytes 98312 | tf_op jit(solution)/shard_map/while/body/eval_jaxpr/ppermute | solution.py:23
  380.9 4.5 collective-permute-start.3
  405.1 2.4 multiply_subtract_fusion.7
  408.1 6.4 %collective-permute-start.2 = (f32[2,16,1,256]{3,2,1,0:T(1,128)S(1)}, f32[2,16,1,256]{3,2,1,0:T(1,128)S(1)}, u32[]{:S(2)}, u32[]{:S(2)}) collective-permute-start(f32[2,16,1,256]{3,2,1,0:T(1,128)S(1)} %pad_maximum_fusion.12), channel_id=1, source_target_pairs={{0,1},{1,2},{2,3},{3,4},{4,5},{5,6},{6,7},{7,8},{8,9},{9,10},{10,1... | collective-permute-start | bytes 98312 | tf_op jit(solution)/shard_map/while/body/eval_jaxpr/ppermute | solution.py:23
  416.4 4.5 collective-permute-start.3
  440.6 2.4 multiply_subtract_fusion.7
  443.6 6.4 %collective-permute-start.2 = (f32[2,16,1,256]{3,2,1,0:T(1,128)S(1)}, f32[2,16,1,256]{3,2,1,0:T(1,128)S(1)}, u32[]{:S(2)}, u32[]{:S(2)}) collective-permute-start(f32[2,16,1,256]{3,2,1,0:T(1,128)S(1)} %pad_maximum_fusion.12), channel_id=1, source_target_pairs={{0,1},{1,2},{2,3},{3,4},{4,5},{5,6},{6,7},{7,8},{8,9},{9,10},{10,1... | collective-permute-start | bytes 98312 | tf_op jit(solution)/shard_map/while/body/eval_jaxpr/ppermute | solution.py:23
  451.9 4.5 collective-permute-start.3
  476.1 2.4 multiply_subtract_fusion.7
  479.1 6.4 %collective-permute-start.2 = (f32[2,16,1,256]{3,2,1,0:T(1,128)S(1)}, f32[2,16,1,256]{3,2,1,0:T(1,128)S(1)}, u32[]{:S(2)}, u32[]{:S(2)}) collective-permute-start(f32[2,16,1,256]{3,2,1,0:T(1,128)S(1)} %pad_maximum_fusion.12), channel_id=1, source_target_pairs={{0,1},{1,2},{2,3},{3,4},{4,5},{5,6},{6,7},{7,8},{8,9},{9,10},{10,1... | collective-permute-start | bytes 98312 | tf_op jit(solution)/shard_map/while/body/eval_jaxpr/ppermute | solution.py:23
  487.4 4.5 collective-permute-start.3
  511.6 2.4 multiply_subtract_fusion.7
  514.6 6.4 %collective-permute-start.2 = (f32[2,16,1,256]{3,2,1,0:T(1,128)S(1)}, f32[2,16,1,256]{3,2,1,0:T(1,128)S(1)}, u32[]{:S(2)}, u32[]{:S(2)}) collective-permute-start(f32[2,16,1,256]{3,2,1,0:T(1,128)S(1)} %pad_maximum_fusion.12), channel_id=1, source_target_pairs={{0,1},{1,2},{2,3},{3,4},{4,5},{5,6},{6,7},{7,8},{8,9},{9,10},{10,1... | collective-permute-start | bytes 98312 | tf_op jit(solution)/shard_map/while/body/eval_jaxpr/ppermute | solution.py:23
  522.9 4.5 collective-permute-start.3
  550.1 6.4 %collective-permute-start.2 = (f32[2,16,1,256]{3,2,1,0:T(1,128)S(1)}, f32[2,16,1,256]{3,2,1,0:T(1,128)S(1)}, u32[]{:S(2)}, u32[]{:S(2)}) collective-permute-start(f32[2,16,1,256]{3,2,1,0:T(1,128)S(1)} %pad_maximum_fusion.12), channel_id=1, source_target_pairs={{0,1},{1,2},{2,3},{3,4},{4,5},{5,6},{6,7},{7,8},{8,9},{9,10},{10,1... | collective-permute-start | bytes 98312 | tf_op jit(solution)/shard_map/while/body/eval_jaxpr/ppermute | solution.py:23
  558.4 4.5 collective-permute-start.3
  573.3 12.1 %psum.28 = f32[16,512]{1,0:T(8,128)S(1)} all-reduce(f32[16,512]{1,0:T(8,128)S(1)} %fusion.27), channel_id=1, replica_groups=mesh['gx_0'=4,'gx_1'=2,'gy_0'=4,'gy_1'=4] {'gx_0'}, use_global_device_ids=true, to_apply=%region_3.4 | all-reduce | flops 8192 | bytes 65536 | tf_op jit(solution)/shard_map/psum | solution.py:27
  585.5 9.4 %psum.29 = f32[16,512]{1,0:T(8,128)S(1)} all-reduce(f32[16,512]{1,0:T(8,128)S(1)} %psum.28), channel_id=1, replica_groups=mesh['gx_0'=4,'gx_1'=2,'gy_0'=4,'gy_1'=4] {'gx_1'}, use_global_device_ids=true, to_apply=%region_4.5 | all-reduce | flops 8192 | bytes 65536 | tf_op jit(solution)/shard_map/psum | solution.py:27
  594.9 20.6 %psum.30 = f32[16,512]{1,0:T(8,128)S(1)} all-reduce(f32[16,512]{1,0:T(8,128)S(1)} %psum.29), channel_id=1, replica_groups=mesh['gx_0'=4,'gx_1'=2,'gy_0'=4,'gy_1'=4] {'gy_0'}, use_global_device_ids=true, to_apply=%region_5.6 | all-reduce | flops 8192 | bytes 65536 | tf_op jit(solution)/shard_map/psum | solution.py:27
  615.5 13.7 %psum.31 = f32[16,512]{1,0:T(8,128)} all-reduce(f32[16,512]{1,0:T(8,128)S(1)} %psum.30), channel_id=1, replica_groups=mesh['gx_0'=4,'gx_1'=2,'gy_0'=4,'gy_1'=4] {'gy_1'}, use_global_device_ids=true, to_apply=%region_6.7 | all-reduce | flops 8192 | bytes 65536 | tf_op jit(solution)/shard_map/psum | solution.py:27
  (1473 shorter events, 372.6 us)
Async XLA Ops:
  10.6 11.8 %collective-permute-start.1 = (f32[2,16,1,256]{3,2,1,0:T(1,128)S(1)}, f32[2,16,1,256]{3,2,1,0:T(1,128)S(1)}, u32[]{:S(2)}, u32[]{:S(2)}) collective-permute-start(f32[2,16,1,256]{3,2,1,0:T(1,128)S(1)} %pad_maximum_fusion.11), channel_id=1, source_target_pairs={{1,0},{2,1},{3,2},{4,3},{5,4},{6,5},{7,6},{8,7},{9,8},{10,9},{11,1... | collective-permute-start | bytes 98312 | tf_op jit(solution)/shard_map/while/body/eval_jaxpr/ppermute | solution.py:23
  12.0 10.5 %collective-permute-start = (f32[2,1,16,256]{3,2,1,0:T(8,128)S(1)}, f32[2,1,16,256]{3,2,1,0:T(8,128)S(1)}, u32[]{:S(2)}, u32[]{:S(2)}) collective-permute-start(f32[2,1,16,256]{3,2,1,0:T(8,128)S(1)} %pad_maximum_fusion.10), channel_id=1, source_target_pairs={{16,0},{32,16},{48,32},{64,48},{80,64},{96,80},{112,96},{17,1},{33... | collective-permute-start | bytes 98312 | tf_op jit(solution)/shard_map/while/body/eval_jaxpr/ppermute | solution.py:23
  25.5 9.6 %collective-permute-start.2 = (f32[2,16,1,256]{3,2,1,0:T(1,128)S(1)}, f32[2,16,1,256]{3,2,1,0:T(1,128)S(1)}, u32[]{:S(2)}, u32[]{:S(2)}) collective-permute-start(f32[2,16,1,256]{3,2,1,0:T(1,128)S(1)} %pad_maximum_fusion.12), channel_id=1, source_target_pairs={{0,1},{1,2},{2,3},{3,4},{4,5},{5,6},{6,7},{7,8},{8,9},{9,10},{10,1... | collective-permute-start | bytes 98312 | tf_op jit(solution)/shard_map/while/body/eval_jaxpr/ppermute | solution.py:23
  44.3 10.5 %collective-permute-start.1 = (f32[2,16,1,256]{3,2,1,0:T(1,128)S(1)}, f32[2,16,1,256]{3,2,1,0:T(1,128)S(1)}, u32[]{:S(2)}, u32[]{:S(2)}) collective-permute-start(f32[2,16,1,256]{3,2,1,0:T(1,128)S(1)} %pad_maximum_fusion.11), channel_id=1, source_target_pairs={{1,0},{2,1},{3,2},{4,3},{5,4},{6,5},{7,6},{8,7},{9,8},{10,9},{11,1... | collective-permute-start | bytes 98312 | tf_op jit(solution)/shard_map/while/body/eval_jaxpr/ppermute | solution.py:23
  45.6 9.2 %collective-permute-start = (f32[2,1,16,256]{3,2,1,0:T(8,128)S(1)}, f32[2,1,16,256]{3,2,1,0:T(8,128)S(1)}, u32[]{:S(2)}, u32[]{:S(2)}) collective-permute-start(f32[2,1,16,256]{3,2,1,0:T(8,128)S(1)} %pad_maximum_fusion.10), channel_id=1, source_target_pairs={{16,0},{32,16},{48,32},{64,48},{80,64},{96,80},{112,96},{17,1},{33... | collective-permute-start | bytes 98312 | tf_op jit(solution)/shard_map/while/body/eval_jaxpr/ppermute | solution.py:23
  57.8 10.7 %collective-permute-start.2 = (f32[2,16,1,256]{3,2,1,0:T(1,128)S(1)}, f32[2,16,1,256]{3,2,1,0:T(1,128)S(1)}, u32[]{:S(2)}, u32[]{:S(2)}) collective-permute-start(f32[2,16,1,256]{3,2,1,0:T(1,128)S(1)} %pad_maximum_fusion.12), channel_id=1, source_target_pairs={{0,1},{1,2},{2,3},{3,4},{4,5},{5,6},{6,7},{7,8},{8,9},{9,10},{10,1... | collective-permute-start | bytes 98312 | tf_op jit(solution)/shard_map/while/body/eval_jaxpr/ppermute | solution.py:23
  77.7 10.5 %collective-permute-start.1 = (f32[2,16,1,256]{3,2,1,0:T(1,128)S(1)}, f32[2,16,1,256]{3,2,1,0:T(1,128)S(1)}, u32[]{:S(2)}, u32[]{:S(2)}) collective-permute-start(f32[2,16,1,256]{3,2,1,0:T(1,128)S(1)} %pad_maximum_fusion.11), channel_id=1, source_target_pairs={{1,0},{2,1},{3,2},{4,3},{5,4},{6,5},{7,6},{8,7},{9,8},{10,9},{11,1... | collective-permute-start | bytes 98312 | tf_op jit(solution)/shard_map/while/body/eval_jaxpr/ppermute | solution.py:23
  79.0 9.2 %collective-permute-start = (f32[2,1,16,256]{3,2,1,0:T(8,128)S(1)}, f32[2,1,16,256]{3,2,1,0:T(8,128)S(1)}, u32[]{:S(2)}, u32[]{:S(2)}) collective-permute-start(f32[2,1,16,256]{3,2,1,0:T(8,128)S(1)} %pad_maximum_fusion.10), channel_id=1, source_target_pairs={{16,0},{32,16},{48,32},{64,48},{80,64},{96,80},{112,96},{17,1},{33... | collective-permute-start | bytes 98312 | tf_op jit(solution)/shard_map/while/body/eval_jaxpr/ppermute | solution.py:23
  91.2 10.7 %collective-permute-start.2 = (f32[2,16,1,256]{3,2,1,0:T(1,128)S(1)}, f32[2,16,1,256]{3,2,1,0:T(1,128)S(1)}, u32[]{:S(2)}, u32[]{:S(2)}) collective-permute-start(f32[2,16,1,256]{3,2,1,0:T(1,128)S(1)} %pad_maximum_fusion.12), channel_id=1, source_target_pairs={{0,1},{1,2},{2,3},{3,4},{4,5},{5,6},{6,7},{7,8},{8,9},{9,10},{10,1... | collective-permute-start | bytes 98312 | tf_op jit(solution)/shard_map/while/body/eval_jaxpr/ppermute | solution.py:23
  111.1 10.5 %collective-permute-start.1 = (f32[2,16,1,256]{3,2,1,0:T(1,128)S(1)}, f32[2,16,1,256]{3,2,1,0:T(1,128)S(1)}, u32[]{:S(2)}, u32[]{:S(2)}) collective-permute-start(f32[2,16,1,256]{3,2,1,0:T(1,128)S(1)} %pad_maximum_fusion.11), channel_id=1, source_target_pairs={{1,0},{2,1},{3,2},{4,3},{5,4},{6,5},{7,6},{8,7},{9,8},{10,9},{11,1... | collective-permute-start | bytes 98312 | tf_op jit(solution)/shard_map/while/body/eval_jaxpr/ppermute | solution.py:23
  112.4 9.2 %collective-permute-start = (f32[2,1,16,256]{3,2,1,0:T(8,128)S(1)}, f32[2,1,16,256]{3,2,1,0:T(8,128)S(1)}, u32[]{:S(2)}, u32[]{:S(2)}) collective-permute-start(f32[2,1,16,256]{3,2,1,0:T(8,128)S(1)} %pad_maximum_fusion.10), channel_id=1, source_target_pairs={{16,0},{32,16},{48,32},{64,48},{80,64},{96,80},{112,96},{17,1},{33... | collective-permute-start | bytes 98312 | tf_op jit(solution)/shard_map/while/body/eval_jaxpr/ppermute | solution.py:23
  124.6 12.2 %collective-permute-start.2 = (f32[2,16,1,256]{3,2,1,0:T(1,128)S(1)}, f32[2,16,1,256]{3,2,1,0:T(1,128)S(1)}, u32[]{:S(2)}, u32[]{:S(2)}) collective-permute-start(f32[2,16,1,256]{3,2,1,0:T(1,128)S(1)} %pad_maximum_fusion.12), channel_id=1, source_target_pairs={{0,1},{1,2},{2,3},{3,4},{4,5},{5,6},{6,7},{7,8},{8,9},{9,10},{10,1... | collective-permute-start | bytes 98312 | tf_op jit(solution)/shard_map/while/body/eval_jaxpr/ppermute | solution.py:23
  146.0 10.5 %collective-permute-start.1 = (f32[2,16,1,256]{3,2,1,0:T(1,128)S(1)}, f32[2,16,1,256]{3,2,1,0:T(1,128)S(1)}, u32[]{:S(2)}, u32[]{:S(2)}) collective-permute-start(f32[2,16,1,256]{3,2,1,0:T(1,128)S(1)} %pad_maximum_fusion.11), channel_id=1, source_target_pairs={{1,0},{2,1},{3,2},{4,3},{5,4},{6,5},{7,6},{8,7},{9,8},{10,9},{11,1... | collective-permute-start | bytes 98312 | tf_op jit(solution)/shard_map/while/body/eval_jaxpr/ppermute | solution.py:23
  147.3 9.2 %collective-permute-start = (f32[2,1,16,256]{3,2,1,0:T(8,128)S(1)}, f32[2,1,16,256]{3,2,1,0:T(8,128)S(1)}, u32[]{:S(2)}, u32[]{:S(2)}) collective-permute-start(f32[2,1,16,256]{3,2,1,0:T(8,128)S(1)} %pad_maximum_fusion.10), channel_id=1, source_target_pairs={{16,0},{32,16},{48,32},{64,48},{80,64},{96,80},{112,96},{17,1},{33... | collective-permute-start | bytes 98312 | tf_op jit(solution)/shard_map/while/body/eval_jaxpr/ppermute | solution.py:23
  159.6 12.8 %collective-permute-start.2 = (f32[2,16,1,256]{3,2,1,0:T(1,128)S(1)}, f32[2,16,1,256]{3,2,1,0:T(1,128)S(1)}, u32[]{:S(2)}, u32[]{:S(2)}) collective-permute-start(f32[2,16,1,256]{3,2,1,0:T(1,128)S(1)} %pad_maximum_fusion.12), channel_id=1, source_target_pairs={{0,1},{1,2},{2,3},{3,4},{4,5},{5,6},{6,7},{7,8},{8,9},{9,10},{10,1... | collective-permute-start | bytes 98312 | tf_op jit(solution)/shard_map/while/body/eval_jaxpr/ppermute | solution.py:23
  181.5 10.5 %collective-permute-start.1 = (f32[2,16,1,256]{3,2,1,0:T(1,128)S(1)}, f32[2,16,1,256]{3,2,1,0:T(1,128)S(1)}, u32[]{:S(2)}, u32[]{:S(2)}) collective-permute-start(f32[2,16,1,256]{3,2,1,0:T(1,128)S(1)} %pad_maximum_fusion.11), channel_id=1, source_target_pairs={{1,0},{2,1},{3,2},{4,3},{5,4},{6,5},{7,6},{8,7},{9,8},{10,9},{11,1... | collective-permute-start | bytes 98312 | tf_op jit(solution)/shard_map/while/body/eval_jaxpr/ppermute | solution.py:23
  182.9 9.2 %collective-permute-start = (f32[2,1,16,256]{3,2,1,0:T(8,128)S(1)}, f32[2,1,16,256]{3,2,1,0:T(8,128)S(1)}, u32[]{:S(2)}, u32[]{:S(2)}) collective-permute-start(f32[2,1,16,256]{3,2,1,0:T(8,128)S(1)} %pad_maximum_fusion.10), channel_id=1, source_target_pairs={{16,0},{32,16},{48,32},{64,48},{80,64},{96,80},{112,96},{17,1},{33... | collective-permute-start | bytes 98312 | tf_op jit(solution)/shard_map/while/body/eval_jaxpr/ppermute | solution.py:23
  195.1 12.8 %collective-permute-start.2 = (f32[2,16,1,256]{3,2,1,0:T(1,128)S(1)}, f32[2,16,1,256]{3,2,1,0:T(1,128)S(1)}, u32[]{:S(2)}, u32[]{:S(2)}) collective-permute-start(f32[2,16,1,256]{3,2,1,0:T(1,128)S(1)} %pad_maximum_fusion.12), channel_id=1, source_target_pairs={{0,1},{1,2},{2,3},{3,4},{4,5},{5,6},{6,7},{7,8},{8,9},{9,10},{10,1... | collective-permute-start | bytes 98312 | tf_op jit(solution)/shard_map/while/body/eval_jaxpr/ppermute | solution.py:23
  217.0 10.5 %collective-permute-start.1 = (f32[2,16,1,256]{3,2,1,0:T(1,128)S(1)}, f32[2,16,1,256]{3,2,1,0:T(1,128)S(1)}, u32[]{:S(2)}, u32[]{:S(2)}) collective-permute-start(f32[2,16,1,256]{3,2,1,0:T(1,128)S(1)} %pad_maximum_fusion.11), channel_id=1, source_target_pairs={{1,0},{2,1},{3,2},{4,3},{5,4},{6,5},{7,6},{8,7},{9,8},{10,9},{11,1... | collective-permute-start | bytes 98312 | tf_op jit(solution)/shard_map/while/body/eval_jaxpr/ppermute | solution.py:23
  218.4 9.2 %collective-permute-start = (f32[2,1,16,256]{3,2,1,0:T(8,128)S(1)}, f32[2,1,16,256]{3,2,1,0:T(8,128)S(1)}, u32[]{:S(2)}, u32[]{:S(2)}) collective-permute-start(f32[2,1,16,256]{3,2,1,0:T(8,128)S(1)} %pad_maximum_fusion.10), channel_id=1, source_target_pairs={{16,0},{32,16},{48,32},{64,48},{80,64},{96,80},{112,96},{17,1},{33... | collective-permute-start | bytes 98312 | tf_op jit(solution)/shard_map/while/body/eval_jaxpr/ppermute | solution.py:23
  230.6 12.8 %collective-permute-start.2 = (f32[2,16,1,256]{3,2,1,0:T(1,128)S(1)}, f32[2,16,1,256]{3,2,1,0:T(1,128)S(1)}, u32[]{:S(2)}, u32[]{:S(2)}) collective-permute-start(f32[2,16,1,256]{3,2,1,0:T(1,128)S(1)} %pad_maximum_fusion.12), channel_id=1, source_target_pairs={{0,1},{1,2},{2,3},{3,4},{4,5},{5,6},{6,7},{7,8},{8,9},{9,10},{10,1... | collective-permute-start | bytes 98312 | tf_op jit(solution)/shard_map/while/body/eval_jaxpr/ppermute | solution.py:23
  252.5 10.5 %collective-permute-start.1 = (f32[2,16,1,256]{3,2,1,0:T(1,128)S(1)}, f32[2,16,1,256]{3,2,1,0:T(1,128)S(1)}, u32[]{:S(2)}, u32[]{:S(2)}) collective-permute-start(f32[2,16,1,256]{3,2,1,0:T(1,128)S(1)} %pad_maximum_fusion.11), channel_id=1, source_target_pairs={{1,0},{2,1},{3,2},{4,3},{5,4},{6,5},{7,6},{8,7},{9,8},{10,9},{11,1... | collective-permute-start | bytes 98312 | tf_op jit(solution)/shard_map/while/body/eval_jaxpr/ppermute | solution.py:23
  253.9 9.2 %collective-permute-start = (f32[2,1,16,256]{3,2,1,0:T(8,128)S(1)}, f32[2,1,16,256]{3,2,1,0:T(8,128)S(1)}, u32[]{:S(2)}, u32[]{:S(2)}) collective-permute-start(f32[2,1,16,256]{3,2,1,0:T(8,128)S(1)} %pad_maximum_fusion.10), channel_id=1, source_target_pairs={{16,0},{32,16},{48,32},{64,48},{80,64},{96,80},{112,96},{17,1},{33... | collective-permute-start | bytes 98312 | tf_op jit(solution)/shard_map/while/body/eval_jaxpr/ppermute | solution.py:23
  266.1 12.8 %collective-permute-start.2 = (f32[2,16,1,256]{3,2,1,0:T(1,128)S(1)}, f32[2,16,1,256]{3,2,1,0:T(1,128)S(1)}, u32[]{:S(2)}, u32[]{:S(2)}) collective-permute-start(f32[2,16,1,256]{3,2,1,0:T(1,128)S(1)} %pad_maximum_fusion.12), channel_id=1, source_target_pairs={{0,1},{1,2},{2,3},{3,4},{4,5},{5,6},{6,7},{7,8},{8,9},{9,10},{10,1... | collective-permute-start | bytes 98312 | tf_op jit(solution)/shard_map/while/body/eval_jaxpr/ppermute | solution.py:23
  288.1 10.5 %collective-permute-start.1 = (f32[2,16,1,256]{3,2,1,0:T(1,128)S(1)}, f32[2,16,1,256]{3,2,1,0:T(1,128)S(1)}, u32[]{:S(2)}, u32[]{:S(2)}) collective-permute-start(f32[2,16,1,256]{3,2,1,0:T(1,128)S(1)} %pad_maximum_fusion.11), channel_id=1, source_target_pairs={{1,0},{2,1},{3,2},{4,3},{5,4},{6,5},{7,6},{8,7},{9,8},{10,9},{11,1... | collective-permute-start | bytes 98312 | tf_op jit(solution)/shard_map/while/body/eval_jaxpr/ppermute | solution.py:23
  289.4 9.2 %collective-permute-start = (f32[2,1,16,256]{3,2,1,0:T(8,128)S(1)}, f32[2,1,16,256]{3,2,1,0:T(8,128)S(1)}, u32[]{:S(2)}, u32[]{:S(2)}) collective-permute-start(f32[2,1,16,256]{3,2,1,0:T(8,128)S(1)} %pad_maximum_fusion.10), channel_id=1, source_target_pairs={{16,0},{32,16},{48,32},{64,48},{80,64},{96,80},{112,96},{17,1},{33... | collective-permute-start | bytes 98312 | tf_op jit(solution)/shard_map/while/body/eval_jaxpr/ppermute | solution.py:23
  301.6 12.8 %collective-permute-start.2 = (f32[2,16,1,256]{3,2,1,0:T(1,128)S(1)}, f32[2,16,1,256]{3,2,1,0:T(1,128)S(1)}, u32[]{:S(2)}, u32[]{:S(2)}) collective-permute-start(f32[2,16,1,256]{3,2,1,0:T(1,128)S(1)} %pad_maximum_fusion.12), channel_id=1, source_target_pairs={{0,1},{1,2},{2,3},{3,4},{4,5},{5,6},{6,7},{7,8},{8,9},{9,10},{10,1... | collective-permute-start | bytes 98312 | tf_op jit(solution)/shard_map/while/body/eval_jaxpr/ppermute | solution.py:23
  323.6 10.5 %collective-permute-start.1 = (f32[2,16,1,256]{3,2,1,0:T(1,128)S(1)}, f32[2,16,1,256]{3,2,1,0:T(1,128)S(1)}, u32[]{:S(2)}, u32[]{:S(2)}) collective-permute-start(f32[2,16,1,256]{3,2,1,0:T(1,128)S(1)} %pad_maximum_fusion.11), channel_id=1, source_target_pairs={{1,0},{2,1},{3,2},{4,3},{5,4},{6,5},{7,6},{8,7},{9,8},{10,9},{11,1... | collective-permute-start | bytes 98312 | tf_op jit(solution)/shard_map/while/body/eval_jaxpr/ppermute | solution.py:23
  324.9 9.2 %collective-permute-start = (f32[2,1,16,256]{3,2,1,0:T(8,128)S(1)}, f32[2,1,16,256]{3,2,1,0:T(8,128)S(1)}, u32[]{:S(2)}, u32[]{:S(2)}) collective-permute-start(f32[2,1,16,256]{3,2,1,0:T(8,128)S(1)} %pad_maximum_fusion.10), channel_id=1, source_target_pairs={{16,0},{32,16},{48,32},{64,48},{80,64},{96,80},{112,96},{17,1},{33... | collective-permute-start | bytes 98312 | tf_op jit(solution)/shard_map/while/body/eval_jaxpr/ppermute | solution.py:23
  337.1 12.8 %collective-permute-start.2 = (f32[2,16,1,256]{3,2,1,0:T(1,128)S(1)}, f32[2,16,1,256]{3,2,1,0:T(1,128)S(1)}, u32[]{:S(2)}, u32[]{:S(2)}) collective-permute-start(f32[2,16,1,256]{3,2,1,0:T(1,128)S(1)} %pad_maximum_fusion.12), channel_id=1, source_target_pairs={{0,1},{1,2},{2,3},{3,4},{4,5},{5,6},{6,7},{7,8},{8,9},{9,10},{10,1... | collective-permute-start | bytes 98312 | tf_op jit(solution)/shard_map/while/body/eval_jaxpr/ppermute | solution.py:23
  359.1 10.5 %collective-permute-start.1 = (f32[2,16,1,256]{3,2,1,0:T(1,128)S(1)}, f32[2,16,1,256]{3,2,1,0:T(1,128)S(1)}, u32[]{:S(2)}, u32[]{:S(2)}) collective-permute-start(f32[2,16,1,256]{3,2,1,0:T(1,128)S(1)} %pad_maximum_fusion.11), channel_id=1, source_target_pairs={{1,0},{2,1},{3,2},{4,3},{5,4},{6,5},{7,6},{8,7},{9,8},{10,9},{11,1... | collective-permute-start | bytes 98312 | tf_op jit(solution)/shard_map/while/body/eval_jaxpr/ppermute | solution.py:23
  360.4 9.2 %collective-permute-start = (f32[2,1,16,256]{3,2,1,0:T(8,128)S(1)}, f32[2,1,16,256]{3,2,1,0:T(8,128)S(1)}, u32[]{:S(2)}, u32[]{:S(2)}) collective-permute-start(f32[2,1,16,256]{3,2,1,0:T(8,128)S(1)} %pad_maximum_fusion.10), channel_id=1, source_target_pairs={{16,0},{32,16},{48,32},{64,48},{80,64},{96,80},{112,96},{17,1},{33... | collective-permute-start | bytes 98312 | tf_op jit(solution)/shard_map/while/body/eval_jaxpr/ppermute | solution.py:23
  372.6 12.8 %collective-permute-start.2 = (f32[2,16,1,256]{3,2,1,0:T(1,128)S(1)}, f32[2,16,1,256]{3,2,1,0:T(1,128)S(1)}, u32[]{:S(2)}, u32[]{:S(2)}) collective-permute-start(f32[2,16,1,256]{3,2,1,0:T(1,128)S(1)} %pad_maximum_fusion.12), channel_id=1, source_target_pairs={{0,1},{1,2},{2,3},{3,4},{4,5},{5,6},{6,7},{7,8},{8,9},{9,10},{10,1... | collective-permute-start | bytes 98312 | tf_op jit(solution)/shard_map/while/body/eval_jaxpr/ppermute | solution.py:23
  394.6 10.5 %collective-permute-start.1 = (f32[2,16,1,256]{3,2,1,0:T(1,128)S(1)}, f32[2,16,1,256]{3,2,1,0:T(1,128)S(1)}, u32[]{:S(2)}, u32[]{:S(2)}) collective-permute-start(f32[2,16,1,256]{3,2,1,0:T(1,128)S(1)} %pad_maximum_fusion.11), channel_id=1, source_target_pairs={{1,0},{2,1},{3,2},{4,3},{5,4},{6,5},{7,6},{8,7},{9,8},{10,9},{11,1... | collective-permute-start | bytes 98312 | tf_op jit(solution)/shard_map/while/body/eval_jaxpr/ppermute | solution.py:23
  395.9 9.2 %collective-permute-start = (f32[2,1,16,256]{3,2,1,0:T(8,128)S(1)}, f32[2,1,16,256]{3,2,1,0:T(8,128)S(1)}, u32[]{:S(2)}, u32[]{:S(2)}) collective-permute-start(f32[2,1,16,256]{3,2,1,0:T(8,128)S(1)} %pad_maximum_fusion.10), channel_id=1, source_target_pairs={{16,0},{32,16},{48,32},{64,48},{80,64},{96,80},{112,96},{17,1},{33... | collective-permute-start | bytes 98312 | tf_op jit(solution)/shard_map/while/body/eval_jaxpr/ppermute | solution.py:23
  408.1 12.8 %collective-permute-start.2 = (f32[2,16,1,256]{3,2,1,0:T(1,128)S(1)}, f32[2,16,1,256]{3,2,1,0:T(1,128)S(1)}, u32[]{:S(2)}, u32[]{:S(2)}) collective-permute-start(f32[2,16,1,256]{3,2,1,0:T(1,128)S(1)} %pad_maximum_fusion.12), channel_id=1, source_target_pairs={{0,1},{1,2},{2,3},{3,4},{4,5},{5,6},{6,7},{7,8},{8,9},{9,10},{10,1... | collective-permute-start | bytes 98312 | tf_op jit(solution)/shard_map/while/body/eval_jaxpr/ppermute | solution.py:23
  430.1 10.5 %collective-permute-start.1 = (f32[2,16,1,256]{3,2,1,0:T(1,128)S(1)}, f32[2,16,1,256]{3,2,1,0:T(1,128)S(1)}, u32[]{:S(2)}, u32[]{:S(2)}) collective-permute-start(f32[2,16,1,256]{3,2,1,0:T(1,128)S(1)} %pad_maximum_fusion.11), channel_id=1, source_target_pairs={{1,0},{2,1},{3,2},{4,3},{5,4},{6,5},{7,6},{8,7},{9,8},{10,9},{11,1... | collective-permute-start | bytes 98312 | tf_op jit(solution)/shard_map/while/body/eval_jaxpr/ppermute | solution.py:23
  431.4 9.2 %collective-permute-start = (f32[2,1,16,256]{3,2,1,0:T(8,128)S(1)}, f32[2,1,16,256]{3,2,1,0:T(8,128)S(1)}, u32[]{:S(2)}, u32[]{:S(2)}) collective-permute-start(f32[2,1,16,256]{3,2,1,0:T(8,128)S(1)} %pad_maximum_fusion.10), channel_id=1, source_target_pairs={{16,0},{32,16},{48,32},{64,48},{80,64},{96,80},{112,96},{17,1},{33... | collective-permute-start | bytes 98312 | tf_op jit(solution)/shard_map/while/body/eval_jaxpr/ppermute | solution.py:23
  443.6 12.8 %collective-permute-start.2 = (f32[2,16,1,256]{3,2,1,0:T(1,128)S(1)}, f32[2,16,1,256]{3,2,1,0:T(1,128)S(1)}, u32[]{:S(2)}, u32[]{:S(2)}) collective-permute-start(f32[2,16,1,256]{3,2,1,0:T(1,128)S(1)} %pad_maximum_fusion.12), channel_id=1, source_target_pairs={{0,1},{1,2},{2,3},{3,4},{4,5},{5,6},{6,7},{7,8},{8,9},{9,10},{10,1... | collective-permute-start | bytes 98312 | tf_op jit(solution)/shard_map/while/body/eval_jaxpr/ppermute | solution.py:23
  465.6 10.5 %collective-permute-start.1 = (f32[2,16,1,256]{3,2,1,0:T(1,128)S(1)}, f32[2,16,1,256]{3,2,1,0:T(1,128)S(1)}, u32[]{:S(2)}, u32[]{:S(2)}) collective-permute-start(f32[2,16,1,256]{3,2,1,0:T(1,128)S(1)} %pad_maximum_fusion.11), channel_id=1, source_target_pairs={{1,0},{2,1},{3,2},{4,3},{5,4},{6,5},{7,6},{8,7},{9,8},{10,9},{11,1... | collective-permute-start | bytes 98312 | tf_op jit(solution)/shard_map/while/body/eval_jaxpr/ppermute | solution.py:23
  466.9 9.2 %collective-permute-start = (f32[2,1,16,256]{3,2,1,0:T(8,128)S(1)}, f32[2,1,16,256]{3,2,1,0:T(8,128)S(1)}, u32[]{:S(2)}, u32[]{:S(2)}) collective-permute-start(f32[2,1,16,256]{3,2,1,0:T(8,128)S(1)} %pad_maximum_fusion.10), channel_id=1, source_target_pairs={{16,0},{32,16},{48,32},{64,48},{80,64},{96,80},{112,96},{17,1},{33... | collective-permute-start | bytes 98312 | tf_op jit(solution)/shard_map/while/body/eval_jaxpr/ppermute | solution.py:23
  479.1 12.8 %collective-permute-start.2 = (f32[2,16,1,256]{3,2,1,0:T(1,128)S(1)}, f32[2,16,1,256]{3,2,1,0:T(1,128)S(1)}, u32[]{:S(2)}, u32[]{:S(2)}) collective-permute-start(f32[2,16,1,256]{3,2,1,0:T(1,128)S(1)} %pad_maximum_fusion.12), channel_id=1, source_target_pairs={{0,1},{1,2},{2,3},{3,4},{4,5},{5,6},{6,7},{7,8},{8,9},{9,10},{10,1... | collective-permute-start | bytes 98312 | tf_op jit(solution)/shard_map/while/body/eval_jaxpr/ppermute | solution.py:23
  501.1 10.5 %collective-permute-start.1 = (f32[2,16,1,256]{3,2,1,0:T(1,128)S(1)}, f32[2,16,1,256]{3,2,1,0:T(1,128)S(1)}, u32[]{:S(2)}, u32[]{:S(2)}) collective-permute-start(f32[2,16,1,256]{3,2,1,0:T(1,128)S(1)} %pad_maximum_fusion.11), channel_id=1, source_target_pairs={{1,0},{2,1},{3,2},{4,3},{5,4},{6,5},{7,6},{8,7},{9,8},{10,9},{11,1... | collective-permute-start | bytes 98312 | tf_op jit(solution)/shard_map/while/body/eval_jaxpr/ppermute | solution.py:23
  502.4 9.2 %collective-permute-start = (f32[2,1,16,256]{3,2,1,0:T(8,128)S(1)}, f32[2,1,16,256]{3,2,1,0:T(8,128)S(1)}, u32[]{:S(2)}, u32[]{:S(2)}) collective-permute-start(f32[2,1,16,256]{3,2,1,0:T(8,128)S(1)} %pad_maximum_fusion.10), channel_id=1, source_target_pairs={{16,0},{32,16},{48,32},{64,48},{80,64},{96,80},{112,96},{17,1},{33... | collective-permute-start | bytes 98312 | tf_op jit(solution)/shard_map/while/body/eval_jaxpr/ppermute | solution.py:23
  514.6 12.8 %collective-permute-start.2 = (f32[2,16,1,256]{3,2,1,0:T(1,128)S(1)}, f32[2,16,1,256]{3,2,1,0:T(1,128)S(1)}, u32[]{:S(2)}, u32[]{:S(2)}) collective-permute-start(f32[2,16,1,256]{3,2,1,0:T(1,128)S(1)} %pad_maximum_fusion.12), channel_id=1, source_target_pairs={{0,1},{1,2},{2,3},{3,4},{4,5},{5,6},{6,7},{7,8},{8,9},{9,10},{10,1... | collective-permute-start | bytes 98312 | tf_op jit(solution)/shard_map/while/body/eval_jaxpr/ppermute | solution.py:23
  536.6 10.5 %collective-permute-start.1 = (f32[2,16,1,256]{3,2,1,0:T(1,128)S(1)}, f32[2,16,1,256]{3,2,1,0:T(1,128)S(1)}, u32[]{:S(2)}, u32[]{:S(2)}) collective-permute-start(f32[2,16,1,256]{3,2,1,0:T(1,128)S(1)} %pad_maximum_fusion.11), channel_id=1, source_target_pairs={{1,0},{2,1},{3,2},{4,3},{5,4},{6,5},{7,6},{8,7},{9,8},{10,9},{11,1... | collective-permute-start | bytes 98312 | tf_op jit(solution)/shard_map/while/body/eval_jaxpr/ppermute | solution.py:23
  537.9 9.2 %collective-permute-start = (f32[2,1,16,256]{3,2,1,0:T(8,128)S(1)}, f32[2,1,16,256]{3,2,1,0:T(8,128)S(1)}, u32[]{:S(2)}, u32[]{:S(2)}) collective-permute-start(f32[2,1,16,256]{3,2,1,0:T(8,128)S(1)} %pad_maximum_fusion.10), channel_id=1, source_target_pairs={{16,0},{32,16},{48,32},{64,48},{80,64},{96,80},{112,96},{17,1},{33... | collective-permute-start | bytes 98312 | tf_op jit(solution)/shard_map/while/body/eval_jaxpr/ppermute | solution.py:23
  550.1 12.8 %collective-permute-start.2 = (f32[2,16,1,256]{3,2,1,0:T(1,128)S(1)}, f32[2,16,1,256]{3,2,1,0:T(1,128)S(1)}, u32[]{:S(2)}, u32[]{:S(2)}) collective-permute-start(f32[2,16,1,256]{3,2,1,0:T(1,128)S(1)} %pad_maximum_fusion.12), channel_id=1, source_target_pairs={{0,1},{1,2},{2,3},{3,4},{4,5},{5,6},{6,7},{7,8},{8,9},{9,10},{10,1... | collective-permute-start | bytes 98312 | tf_op jit(solution)/shard_map/while/body/eval_jaxpr/ppermute | solution.py:23
  (440 other events, 2516.3 us)
where the time goes:
time: 644 us; the launch traced here: 631 us
  starting transfers between devices  219 us (34%)
  local copies, waits for them, and re-layouts  161 us (25%)
  other arithmetic  119 us (18%)
  blocking collectives  55.7 us (9%)
  matrix products  52 us (8%)
  waiting for transfers between devices  15.8 us (2%)
  loops' own time  7.44 us (1%)
    ppermute x64, starting transfers between devices, passed_along(): return lax.ppermute(block, axis, route)  219 us
    slice x96, local copies, waits for them, and re-layouts, difference(): lax.slice_in_dim(values, 1, length, axis=axis)  73.5 us
    psum x4, blocking collectives, over_axes(): return functools.reduce(lax.psum, axes, value)  55.7 us
    sub x48, other arithmetic, turn_parts(): field_h[number] - courant * rotation[number]  50.1 us
    add x16, other arithmetic, turn_parts(): field_e[1] + factor * rotation[1]  38.5 us
    while x832, local copies, waits for them, and re-layouts  37.5 us
    dot_general x16, matrix products, inject(): lax.dot_general(weighted, depth_table, (((0,), (0,)), ((), ())), precisio...  30.3 us
    dynamic_update_slice x16, local copies, waits for them, and re-layouts, note_power(): return lax.dynamic_update_slice_in_dim(record, drive[None, :], index, 0)  21.4 us
  transfers between devices with their start and end apart: 64, of which 16 were waited for; matrix products, arithmetic and copies ran while one was open for 21% of the time, Pallas kernels for 0%

commit v1 on v0

v1 whole, which is shorter than its diff:
```python
import functools

import jax
import jax.numpy as jnp
from jax import lax
from jax.experimental import pallas as pl
from jax.experimental.pallas import tpu as pltpu
from jax.sharding import PartitionSpec as P

MESH = pl.DeviceIdType.MESH
S = 0.55
KEEP = (0.0, 0.92, 0.75, 0.45)
TAKE = (0.0, -0.06, -0.18, -0.35)
BF = jnp.bfloat16


def table(grades, values):
    out = jnp.zeros(grades.shape, jnp.float32)
    for level in range(1, 4):
        out = jnp.where(grades == level, values[level], out)
    return out


def halves(value):
    high = value.astype(BF)
    low = (value - high.astype(jnp.float32)).astype(BF)
    return high, low


def dot_nt(a, b):
    return lax.dot_general(a, b, (((1,), (1,)), ((), ())), preferred_element_type=jnp.float32)


def dot_nn(a, b):
    return jnp.dot(a, b, preferred_element_type=jnp.float32)


def kernel(
    shape, steps,
    live_ref, e_hbm, h_hbm, me_hbm, mh_hbm, g_hbm, p_hbm, cell_ref, port_ref, inj_ref, wave_ref,
    eo_hbm, ho_hbm, pw_ref,
    E, H, ME, MH, G, KP, TK, FC, PR, cellT, depthT, curT, rec, J,
    ey_send, hy_send, ey_recv, hy_recv,
    load_sem, store_sem, send_sem, recv_sem,
):
    nx, ny, nz = shape
    gx, gy = lax.axis_index("gx"), lax.axis_index("gy")
    last_x, last_y = lax.axis_size("gx") - 1, lax.axis_size("gy") - 1
    x_low, x_high = gx > 0, gx < last_x
    y_low, y_high = gy > 0, gy < last_y
    sides = (
        (x_low, (gx - 1, gy)),
        (x_high, (gx + 1, gy)),
        (y_low, (gx, gy - 1)),
        (y_high, (gx, gy + 1)),
    )
    loads = [
        pltpu.make_async_copy(e_hbm, E.at[:, 0:nx], load_sem.at[0]),
        pltpu.make_async_copy(h_hbm, H.at[:, 1 : nx + 1], load_sem.at[1]),
        pltpu.make_async_copy(me_hbm, ME, load_sem.at[2]),
        pltpu.make_async_copy(mh_hbm, MH, load_sem.at[3]),
        pltpu.make_async_copy(g_hbm, G, load_sem.at[4]),
        pltpu.make_async_copy(p_hbm, PR, load_sem.at[5]),
    ]
    for copy in loads:
        copy.start()
    zero_plane = jnp.zeros((ny, nz), jnp.float32)
    for c in range(3):
        E[c, nx] = zero_plane
        H[c, 0] = zero_plane
    ey_recv[...] = jnp.zeros_like(ey_recv)
    hy_recv[...] = jnp.zeros_like(hy_recv)

    barrier = pltpu.get_barrier_semaphore()
    for ok, target in sides:
        @pl.when(ok)
        def _():
            pl.semaphore_signal(barrier, inc=1, device_id=target, device_id_type=MESH)

    slots = cell_ref.shape[1]
    cell = (cell_ref[0:1, :] - gx * nx) * ny + (cell_ref[1:2, :] - gy * ny)
    cellT[...] = (
        lax.broadcasted_iota(jnp.int32, (nx * ny, slots), 0) == cell
    ).astype(jnp.float32)
    depthT[...] = (
        lax.broadcasted_iota(jnp.int32, (nz, slots), 0) == cell_ref[2:3, :]
    ).astype(jnp.float32).astype(BF)
    live = lax.broadcasted_iota(jnp.int32, (1, slots), 1) < live_ref[0]
    curT[...] = jnp.where(live, dot_nt(wave_ref[...], inj_ref[...]), 0.0)

    for copy in loads:
        copy.wait()

    @pl.loop(0, nx)
    def _(x):
        for d in range(3):
            grades = G[d, x]
            KP[d, x] = table(grades, KEEP)
            TK[d, x] = table(grades, TAKE)
        FC[x] = S / PR[x]

    pl.semaphore_wait(barrier, sum(ok.astype(jnp.int32) for ok, _ in sides))

    row = lax.broadcasted_iota(jnp.int32, (ny, nz), 0)
    lane = lax.broadcasted_iota(jnp.int32, (ny, nz), 1)

    def next_y(v):
        return jnp.where(row == ny - 1, 0.0, pltpu.roll(v, ny - 1, 0))

    def prev_y(v):
        return jnp.where(row == 0, 0.0, pltpu.roll(v, 1, 0))

    def next_z(v):
        return jnp.where(lane == nz - 1, 0.0, pltpu.roll(v, nz - 1, 1))

    def prev_z(v):
        return jnp.where(lane == 0, 0.0, pltpu.roll(v, 1, 1))

    def terms(slopes, memory, x):
        out = []
        for k, (slope, d) in enumerate(zip(slopes, (1, 2, 2, 0, 0, 1))):
            carried = KP[d, x] * memory[k, x] + TK[d, x] * slope
            memory[k, x] = carried
            out.append(slope + carried)
        return out

    def h_plane(x):
        ex, ey, ez = E[0, x], E[1, x], E[2, x]
        t = terms(
            (
                next_y(ez) - ez,
                next_z(ey) - ey,
                next_z(ex) - ex,
                E[2, x + 1] - ez,
                E[1, x + 1] - ey,
                next_y(ex) - ex,
            ),
            ME,
            x,
        )
        for c in range(3):
            H[c, x + 1] = H[c, x + 1] - S * (t[2 * c] - t[2 * c + 1])

    def e_plane(x):
        hx, hy, hz = H[0, x + 1], H[1, x + 1], H[2, x + 1]
        t = terms(
            (
                hz - prev_y(hz),
                hy - prev_z(hy),
                hx - prev_z(hx),
                hz - H[2, x],
                hy - H[1, x],
                hx - prev_y(hx),
            ),
            MH,
            x,
        )
        factor = FC[x]
        E[0, x] = E[0, x] + factor * (t[0] - t[1])
        E[1, x] = E[1, x] + factor * (t[2] - t[3])
        source = J[pl.ds(pl.multiple_of(x * ny, ny), ny), :]
        E[2, x] = E[2, x] + factor * (t[4] - t[5]) - source

    def remote(number, source, target_ref, target):
        return pltpu.make_async_remote_copy(
            src_ref=source,
            dst_ref=target_ref,
            send_sem=send_sem.at[number],
            recv_sem=recv_sem.at[number],
            device_id=target,
            device_id_type=MESH,
        )

    ex_copy = remote(0, E.at[1:3, 0], E.at[1:3, nx], (gx - 1, gy))
    ey_copy = remote(1, ey_send, ey_recv, (gx, gy - 1))
    hx_copy = remote(2, H.at[1:3, nx], H.at[1:3, 0], (gx + 1, gy))
    hy_copy = remote(3, hy_send, hy_recv, (gx, gy + 1))

    def drive(t):
        high, low = halves(E[2, 0:nx].reshape(nx * ny, nz))
        picked = dot_nn(high, depthT[...]) + dot_nn(low, depthT[...])
        value = jnp.sum(picked * cellT[...], axis=0, keepdims=True)
        rec[pl.ds(t, 1), :] = value * curT[pl.ds(t, 1), :]

    def sources(t):
        high, low = halves(S * curT[pl.ds(t, 1), :])
        mask = cellT[...].astype(BF)
        J[...] = dot_nt(mask * high, depthT[...]) + dot_nt(mask * low, depthT[...])

    @pl.loop(0, steps)
    def _(t):
        @pl.loop(0, nx)
        def _(x):
            ey_send[0, pl.ds(x, 1), :] = E[0, x, 0:1, :]
            ey_send[1, pl.ds(x, 1), :] = E[2, x, 0:1, :]

        @pl.when(x_low)
        def _():
            ex_copy.start()

        @pl.when(y_low)
        def _():
            ey_copy.start()

        @pl.loop(0, nx - 1)
        def _(x):
            h_plane(x)

        @pl.when(t > 0)
        def _():
            drive(t - 1)

        @pl.when(x_high)
        def _():
            ex_copy.wait_recv()

        h_plane(nx - 1)

        @pl.when(y_high)
        def _():
            ey_copy.wait_recv()

        @pl.loop(0, nx)
        def _(x):
            last = slice(ny - 1, ny)
            keep_take = TK[1, x, last, :]
            gx_row, gz_row = ey_recv[0, pl.ds(x, 1), :], ey_recv[1, pl.ds(x, 1), :]
            moved_z, moved_x = keep_take * gz_row, keep_take * gx_row
            ME[0, x, last, :] = ME[0, x, last, :] + moved_z
            ME[5, x, last, :] = ME[5, x, last, :] + moved_x
            new_x = H[0, x + 1, last, :] - S * (gz_row + moved_z)
            new_z = H[2, x + 1, last, :] + S * (gx_row + moved_x)
            H[0, x + 1, last, :] = new_x
            H[2, x + 1, last, :] = new_z
            hy_send[0, pl.ds(x, 1), :] = new_x
            hy_send[1, pl.ds(x, 1), :] = new_z

        @pl.when(x_high)
        def _():
            hx_copy.start()

        @pl.when(y_high)
        def _():
            hy_copy.start()

        sources(t)

        @pl.when(x_low)
        def _():
            ex_copy.wait_send()

        @pl.when(y_low)
        def _():
            ey_copy.wait_send()

        @pl.loop(1, nx)
        def _(x):
            e_plane(x)

        @pl.when(x_low)
        def _():
            hx_copy.wait_recv()

        e_plane(0)

        @pl.when(y_low)
        def _():
            hy_copy.wait_recv()

        @pl.loop(0, nx)
        def _(x):
            first = slice(0, 1)
            take_row, factor = TK[1, x, first, :], FC[x, first, :]
            hx_row, hz_row = hy_recv[0, pl.ds(x, 1), :], hy_recv[1, pl.ds(x, 1), :]
            moved_z, moved_x = take_row * hz_row, take_row * hx_row
            MH[0, x, first, :] = MH[0, x, first, :] - moved_z
            MH[5, x, first, :] = MH[5, x, first, :] - moved_x
            E[0, x, first, :] = E[0, x, first, :] - factor * (hz_row + moved_z)
            E[2, x, first, :] = E[2, x, first, :] + factor * (hx_row + moved_x)

        @pl.when(x_high)
        def _():
            hx_copy.wait_send()

        @pl.when(y_high)
        def _():
            hy_copy.wait_send()

    stores = [
        pltpu.make_async_copy(E.at[:, 0:nx], eo_hbm, store_sem.at[0]),
        pltpu.make_async_copy(H.at[:, 1 : nx + 1], ho_hbm, store_sem.at[1]),
    ]
    for copy in stores:
        copy.start()
    drive(steps - 1)
    ports = pw_ref.shape[1]
    members = (
        lax.broadcasted_iota(jnp.int32, (ports, slots), 0) == port_ref[...]
    ).astype(jnp.float32).astype(BF)
    high, low = halves(rec[...])
    pw_ref[...] = dot_nt(high, members) + dot_nt(low, members)
    for copy in stores:
        copy.wait()


def local(
    electric, magnetic, aux_electric, aux_magnetic, grades, permittivity,
    dipole_cell, dipole_port, live_count, injection, waveform,
):
    shape = electric.shape[1:]
    nx, ny, nz = shape
    slots = dipole_cell.shape[1]
    ports, steps = waveform.shape
    f32 = jnp.float32
    anywhere = pl.BlockSpec(memory_space=pl.ANY)
    vmem = pl.BlockSpec(memory_space=pltpu.VMEM)
    electric, magnetic, partial = pl.pallas_call(
        functools.partial(kernel, shape, steps),
        out_shape=(
            jax.ShapeDtypeStruct(electric.shape, f32),
            jax.ShapeDtypeStruct(magnetic.shape, f32),
            jax.ShapeDtypeStruct((steps, ports), f32),
        ),
        in_specs=[pl.BlockSpec(memory_space=pltpu.SMEM)] + [anywhere] * 6 + [vmem] * 4,
        out_specs=(anywhere, anywhere, vmem),
        scratch_shapes=[
            pltpu.VMEM((3, nx + 1, ny, nz), f32),
            pltpu.VMEM((3, nx + 1, ny, nz), f32),
            pltpu.VMEM((6, nx, ny, nz), f32),
            pltpu.VMEM((6, nx, ny, nz), f32),
            pltpu.VMEM((3, nx, ny, nz), jnp.int32),
            pltpu.VMEM((3, nx, ny, nz), f32),
            pltpu.VMEM((3, nx, ny, nz), f32),
            pltpu.VMEM((nx, ny, nz), f32),
            pltpu.VMEM((nx, ny, nz), f32),
            pltpu.VMEM((nx * ny, slots), f32),
            pltpu.VMEM((nz, slots), BF),
            pltpu.VMEM((steps, slots), f32),
            pltpu.VMEM((steps, slots), f32),
            pltpu.VMEM((nx * ny, nz), f32),
            pltpu.VMEM((2, nx, nz), f32),
            pltpu.VMEM((2, nx, nz), f32),
            pltpu.VMEM((2, nx, nz), f32),
            pltpu.VMEM((2, nx, nz), f32),
            pltpu.SemaphoreType.DMA((6,)),
            pltpu.SemaphoreType.DMA((2,)),
            pltpu.SemaphoreType.DMA((4,)),
            pltpu.SemaphoreType.DMA((4,)),
        ],
        compiler_params=pltpu.CompilerParams(
            collective_id=0, has_side_effects=True, vmem_limit_bytes=48 * 1024 * 1024
        ),
    )(
        live_count, electric, magnetic, aux_electric, aux_magnetic, grades, permittivity,
        dipole_cell, dipole_port.reshape(1, slots), injection, waveform.T,
    )
    return electric, magnetic, lax.psum(partial, ("gx", "gy"))


def solution(mesh):
    block = P(None, "gx", "gy", None)
    each = ("gx", "gy")
    return jax.shard_map(
        local,
        mesh=mesh,
        in_specs=(
            block, block, block, block, block, P("gx", "gy", None),
            P(None, each), P(each), P(each), P(each, None), P(),
        ),
        out_specs=(block, block, P()),
        check_vma=False,
    )
```

time: 644 us -> 216 us (0.34); the launches traced: 631 us -> 215 us
  starting transfers between devices: 219 us -> 0 us
  local copies, waits for them, and re-layouts: 161 us -> 9.23 us
  Pallas kernels: 0 us -> 128 us
  other arithmetic: 119 us -> 0 us
  matrix products: 52 us -> 0 us
  blocking collectives: 55.7 us -> 77 us
  waiting for transfers between devices: 15.8 us -> 0 us
  loops' own time: 7.44 us -> 0 us
    ppermute x64 -> x0, starting transfers between devices: 219 us -> none  [passed_along(): return lax.ppermute(block, axis, route)]
    pallas_call x0 -> x1, Pallas kernels: none -> 128 us  [local(): pl.pallas_call(functools.partial(kernel, shape, steps), out_shape=(jax.Sh...]
    slice x128 -> x0, local copies, waits for them, and re-layouts: 84.9 us -> none  [the longest x96 73.5 us: difference(): lax.slice_in_dim(values, 1, length, axis=axis)]
    sub x64 -> x0, other arithmetic: 56.7 us -> none  [the longest x48 50.1 us: turn_parts(): field_h[number] - courant * rotation[number]]
    dot_general x34 -> x0, matrix products: 52 us -> none  [the longest x16 30.3 us: inject(): lax.dot_general(weighted, depth_table, (((0,), (0,)), ((), ())), precisio...]
    add x34 -> x0, other arithmetic: 44.9 us -> none  [the longest x16 38.5 us: turn_parts(): field_e[1] + factor * rotation[1]]
    while x832 -> x0, local copies, waits for them, and re-layouts: 37.5 us -> none
    dynamic_update_slice x16 -> x0, local copies, waits for them, and re-layouts: 21.4 us -> none  [note_power(): return lax.dynamic_update_slice_in_dim(record, drive[None, :], index, 0)]
  transfers between devices with their start and end apart: 64 -> 0, of which waited for: 16 -> 0; matrix products, arithmetic and copies ran while one was open for 21% -> 0% of each run, Pallas kernels for 0% -> 0%
where the time goes in v1:
time: 216 us; the launch traced here: 215 us
  Pallas kernels  128 us (59%)
  blocking collectives  77 us (36%)
  local copies, waits for them, and re-layouts  9.23 us (4%)
    pallas_call x1, Pallas kernels, local(): pl.pallas_call(functools.partial(kernel, shape, steps), out_shape=(jax.Sh...  128 us
    psum x1, blocking collectives, local(): return (electric, magnetic, lax.psum(partial, ('gx', 'gy')))  77 us
    unnamed x18, local copies, waits for them, and re-layouts  9.23 us

profile of v1, /device:TPU:1, one launch (start us, length us, event | category | flops | bytes accessed | tf_op | source)
XLA Modules:
  0.0 215.3 jit_solution(2090020361884986893)
XLA Ops:
  1.3 0.0 copy-start
  1.3 1.1 copy-done
  2.4 0.0 copy-start.1
  2.4 1.1 copy-done.1
  3.5 0.0 copy-start.2
  3.6 1.1 copy-done.2
  4.7 0.0 copy-start.3
  4.7 1.0 copy-done.3
  5.7 0.0 copy-start.4
  5.7 0.9 copy-done.4
  6.7 0.0 copy-start.5
  6.7 0.7 copy-done.5
  7.4 0.0 copy-start.6
  7.4 0.7 copy-done.6
  8.1 0.0 copy-start.7
  8.1 0.7 copy-done.7
  8.8 127.8 %shard_map.130 = (f32[3,16,16,256]{3,2,1,0:T(8,128)S(1)}, f32[3,16,16,256]{3,2,1,0:T(8,128)S(1)}, f32[16,512]{1,0:T(8,128)S(1)}) custom-call(s32[1]{0:T(128)S(6)} %copy.16.live_ref, f32[3,16,16,256]{3,2,1,0:T(8,128)S(1)} %copy-done, f32[3,16,16,256]{3,2,1,0:T(8,128)S(1)} %copy-done.1, f32[6,16,16,256]{3,2,1,0:T(8,128)} %me_hbm.1, f32[6,16,16,256]{3,2,1,0:T(8,128)} %mh_hbm.1, ...), custom_call_target="tpu_custom_call" | custom-call | tf_op jit(solution)/shard_map/pallas_call | solution.py:317
  136.5 77.0 %psum.7 = f32[16,512]{1,0:T(8,128)} all-reduce(f32[16,512]{1,0:T(8,128)S(1)} %get-tuple-element.8), channel_id=1, replica_groups=mesh['gx'=8,'gy'=16] {'gx','gy'}, use_global_device_ids=true, to_apply=%region_0.0 | all-reduce | flops 8192 | bytes 65536 | tf_op jit(solution)/shard_map/psum | solution.py:357
  213.5 0.9 copy.17
  214.4 0.9 copy.18
Async XLA Ops:
  1.3 1.1 copy-start
  2.4 1.1 copy-start.1
  3.5 1.1 copy-start.2
  4.7 1.0 copy-start.3
  5.7 0.9 copy-start.4
  6.7 0.7 copy-start.5
  7.4 0.7 copy-start.6
  8.1 0.7 copy-start.7

commit v2 on v1

--- a/solution.py
+++ b/solution.py
@@ -37,11 +37,12 @@
 
 def kernel(
     shape, steps,
-    live_ref, e_hbm, h_hbm, me_hbm, mh_hbm, g_hbm, p_hbm, cell_ref, port_ref, inj_ref, wave_ref,
+    live_ref, e_hbm, h_hbm, me_hbm, mh_hbm, g_hbm, p_hbm, cell_hbm, port_hbm, inj_hbm, wave_hbm,
     eo_hbm, ho_hbm, pw_ref,
     E, H, ME, MH, G, KP, TK, FC, PR, cellT, depthT, curT, rec, J,
-    ey_send, hy_send, ey_recv, hy_recv,
-    load_sem, store_sem, send_sem, recv_sem,
+    ey_send, hy_send, ey_recv, hy_recv, cell_ref, port_ref, inj_ref, wave_ref,
+    part, half, ring, whole,
+    load_sem, store_sem, send_sem, recv_sem, pair_send, pair_recv, ring_send, ring_recv,
 ):
     nx, ny, nz = shape
     gx, gy = lax.axis_index("gx"), lax.axis_index("gy")
@@ -54,6 +55,25 @@
         (y_low, (gx, gy - 1)),
         (y_high, (gx, gy + 1)),
     )
+    core, chip_x, chip_y, chip_z = gx % 2, gx // 2, gy // 4, gy % 4
+    partner = (chip_x * 2 + 1 - core, gy)
+    places = (chip_x, chip_y, chip_z)
+
+    def fellow(axis, shift):
+        if axis == 0:
+            return ((chip_x + shift) % 4 * 2 + core, gy)
+        if axis == 1:
+            return (gx, (chip_y + shift) % 4 * 4 + chip_z)
+        return (gx, chip_y * 4 + (chip_z + shift) % 4)
+
+    small = [
+        pltpu.make_async_copy(cell_hbm, cell_ref, load_sem.at[6]),
+        pltpu.make_async_copy(port_hbm, port_ref, load_sem.at[7]),
+        pltpu.make_async_copy(inj_hbm, inj_ref, load_sem.at[8]),
+        pltpu.make_async_copy(wave_hbm, wave_ref, load_sem.at[9]),
+    ]
+    for copy in small:
+        copy.start()
     loads = [
         pltpu.make_async_copy(e_hbm, E.at[:, 0:nx], load_sem.at[0]),
         pltpu.make_async_copy(h_hbm, H.at[:, 1 : nx + 1], load_sem.at[1]),
@@ -77,6 +97,11 @@
         def _():
             pl.semaphore_signal(barrier, inc=1, device_id=target, device_id_type=MESH)
 
+    friends = [partner] + [fellow(axis, shift) for axis in range(3) for shift in range(1, 4)]
+    for target in friends:
+        pl.semaphore_signal(barrier, inc=1, device_id=target, device_id_type=MESH)
+    for copy in small:
+        copy.wait()
     slots = cell_ref.shape[1]
     cell = (cell_ref[0:1, :] - gx * nx) * ny + (cell_ref[1:2, :] - gy * ny)
     cellT[...] = (
@@ -99,7 +124,7 @@
             TK[d, x] = table(grades, TAKE)
         FC[x] = S / PR[x]
 
-    pl.semaphore_wait(barrier, sum(ok.astype(jnp.int32) for ok, _ in sides))
+    pl.semaphore_wait(barrier, sum(ok.astype(jnp.int32) for ok, _ in sides) + len(friends))
 
     row = lax.broadcasted_iota(jnp.int32, (ny, nz), 0)
     lane = lax.broadcasted_iota(jnp.int32, (ny, nz), 1)
@@ -293,12 +318,66 @@
     for copy in stores:
         copy.start()
     drive(steps - 1)
-    ports = pw_ref.shape[1]
+    rows, ports = half.shape
     members = (
         lax.broadcasted_iota(jnp.int32, (ports, slots), 0) == port_ref[...]
     ).astype(jnp.float32).astype(BF)
     high, low = halves(rec[...])
-    pw_ref[...] = dot_nt(high, members) + dot_nt(low, members)
+    total = dot_nt(high, members) + dot_nt(low, members)
+    part[0] = total[0:rows]
+    part[1] = total[rows : 2 * rows]
+
+    def swap(number, source, target_ref):
+        return pltpu.make_async_remote_copy(
+            src_ref=source,
+            dst_ref=target_ref,
+            send_sem=pair_send.at[number],
+            recv_sem=pair_recv.at[number],
+            device_id=partner,
+            device_id_type=MESH,
+        )
+
+    def send(axis, shift):
+        return pltpu.make_async_remote_copy(
+            src_ref=ring.at[axis, places[axis]],
+            dst_ref=ring.at[axis, places[axis]],
+            send_sem=ring_send.at[axis, shift],
+            recv_sem=ring_recv.at[axis, shift],
+            device_id=fellow(axis, shift),
+            device_id_type=MESH,
+        )
+
+    def arrival(axis, shift):
+        slot = (places[axis] + 4 - shift) % 4
+        return pltpu.make_async_remote_copy(
+            src_ref=ring.at[axis, slot],
+            dst_ref=ring.at[axis, slot],
+            send_sem=ring_send.at[axis, shift],
+            recv_sem=ring_recv.at[axis, shift],
+            device_id=fellow(axis, shift),
+            device_id_type=MESH,
+        )
+
+    trade = swap(0, part.at[1 - core], half)
+    trade.start()
+    trade.wait()
+    value = part[core] + half[...]
+    for axis in range(3):
+        ring[axis, places[axis]] = value
+        for shift in range(1, 4):
+            send(axis, shift).start()
+        for shift in range(1, 4):
+            arrival(axis, shift).wait_recv()
+        value = (ring[axis, 0] + ring[axis, 1]) + (ring[axis, 2] + ring[axis, 3])
+    whole[core] = value
+    trade = swap(1, whole.at[core], whole.at[core])
+    trade.start()
+    for axis in range(3):
+        for shift in range(1, 4):
+            send(axis, shift).wait_send()
+    trade.wait()
+    pw_ref[0:rows] = whole[0]
+    pw_ref[rows : 2 * rows] = whole[1]
     for copy in stores:
         copy.wait()
 
@@ -314,14 +393,15 @@
     f32 = jnp.float32
     anywhere = pl.BlockSpec(memory_space=pl.ANY)
     vmem = pl.BlockSpec(memory_space=pltpu.VMEM)
-    electric, magnetic, partial = pl.pallas_call(
+    half = (steps // 2, ports)
+    return pl.pallas_call(
         functools.partial(kernel, shape, steps),
         out_shape=(
             jax.ShapeDtypeStruct(electric.shape, f32),
             jax.ShapeDtypeStruct(magnetic.shape, f32),
             jax.ShapeDtypeStruct((steps, ports), f32),
         ),
-        in_specs=[pl.BlockSpec(memory_space=pltpu.SMEM)] + [anywhere] * 6 + [vmem] * 4,
+        in_specs=[pl.BlockSpec(memory_space=pltpu.SMEM)] + [anywhere] * 10,
         out_specs=(anywhere, anywhere, vmem),
         scratch_shapes=[
             pltpu.VMEM((3, nx + 1, ny, nz), f32),
@@ -342,19 +422,30 @@
             pltpu.VMEM((2, nx, nz), f32),
             pltpu.VMEM((2, nx, nz), f32),
             pltpu.VMEM((2, nx, nz), f32),
-            pltpu.SemaphoreType.DMA((6,)),
+            pltpu.VMEM((3, slots), jnp.int32),
+            pltpu.VMEM((1, slots), jnp.int32),
+            pltpu.VMEM((slots, ports), BF),
+            pltpu.VMEM((steps, ports), BF),
+            pltpu.VMEM((2,) + half, f32),
+            pltpu.VMEM(half, f32),
+            pltpu.VMEM((3, 4) + half, f32),
+            pltpu.VMEM((2,) + half, f32),
+            pltpu.SemaphoreType.DMA((10,)),
             pltpu.SemaphoreType.DMA((2,)),
             pltpu.SemaphoreType.DMA((4,)),
             pltpu.SemaphoreType.DMA((4,)),
+            pltpu.SemaphoreType.DMA((2,)),
+            pltpu.SemaphoreType.DMA((2,)),
+            pltpu.SemaphoreType.DMA((3, 4)),
+            pltpu.SemaphoreType.DMA((3, 4)),
         ],
         compiler_params=pltpu.CompilerParams(
-            collective_id=0, has_side_effects=True, vmem_limit_bytes=48 * 1024 * 1024
+            collective_id=0, has_side_effects=True, vmem_limit_bytes=67_043_328
         ),
     )(
         live_count, electric, magnetic, aux_electric, aux_magnetic, grades, permittivity,
         dipole_cell, dipole_port.reshape(1, slots), injection, waveform.T,
     )
-    return electric, magnetic, lax.psum(partial, ("gx", "gy"))
 
 
 def solution(mesh):

time: 216 us -> 159 us (0.74)
  blocking collectives: 77 us -> 0 us
  Pallas kernels: 128 us -> 154 us
  local copies, waits for them, and re-layouts: 9.23 us -> 3.64 us
    psum x1 -> x0, blocking collectives: 77 us -> none  [local(): return (electric, magnetic, lax.psum(partial, ('gx', 'gy')))]
    pallas_call x1, Pallas kernels: 128 us -> 154 us  [local(): pl.pallas_call(functools.partial(kernel, shape, steps), out_shape=(jax.Sh...]
    unnamed x18 -> x7, local copies, waits for them, and re-layouts: 9.23 us -> 3.64 us
where the time goes in v2:
time: 159 us
  Pallas kernels  154 us (97%)
  local copies, waits for them, and re-layouts  3.64 us (2%)
    pallas_call x1, Pallas kernels, local(): pl.pallas_call(functools.partial(kernel, shape, steps), out_shape=(jax.Sh...  154 us
    unnamed x7, local copies, waits for them, and re-layouts  3.64 us

profile of v2, /device:TPU:1, one launch (start us, length us, event | category | flops | bytes accessed | tf_op | source)
XLA Modules:
  0.0 158.8 jit_solution(14647359339264036815)
XLA Ops:
  1.3 153.9 %shard_map.130 = (f32[3,16,16,256]{3,2,1,0:T(8,128)}, f32[3,16,16,256]{3,2,1,0:T(8,128)}, f32[16,512]{1,0:T(8,128)}) custom-call(s32[1]{0:T(128)S(6)} %copy.17.live_ref, f32[3,16,16,256]{3,2,1,0:T(8,128)} %e_hbm.1, f32[3,16,16,256]{3,2,1,0:T(8,128)} %h_hbm.1, f32[6,16,16,256]{3,2,1,0:T(8,128)} %me_hbm.1, f32[6,16,16,256]{3,2,1,0:T(8,128)} %mh_hbm.1, ...), custom_call_target="tpu_custom_call" | custom-call | tf_op jit(solution)/shard_map/pallas_call | solution.py:397
  155.2 0.0 copy-start
  155.2 0.0 copy-start.1
  155.2 2.1 %copy.18 = f32[3,16,16,256]{3,2,1,0:T(8,128)} copy(f32[3,16,16,256]{3,2,1,0:T(8,128)} %get-tuple-element.6) | data formatting | bytes 1572864
  157.3 0.0 copy-done
  157.3 0.9 copy.19
  158.2 0.0 copy-done.1
  158.2 0.6 copy.20
Async XLA Ops:
  155.2 2.2 %copy-start = (f32[3,16,16,256]{3,2,1,0:T(8,128)S(1)}, f32[3,16,16,256]{3,2,1,0:T(8,128)}, u32[]{:S(2)}) copy-start(f32[3,16,16,256]{3,2,1,0:T(8,128)} %get-tuple-element.7) | copy-start | bytes 2359300
  155.2 3.0 %copy-start.1 = (f32[16,512]{1,0:T(8,128)S(1)}, f32[16,512]{1,0:T(8,128)}, u32[]{:S(2)}) copy-start(f32[16,512]{1,0:T(8,128)} %get-tuple-element.8) | copy-start | bytes 98308

commit v3 on v2

v3 whole, which is shorter than its diff:
```python
import functools

import jax
import jax.numpy as jnp
from jax import lax
from jax.experimental import pallas as pl
from jax.experimental.pallas import tpu as pltpu
from jax.sharding import PartitionSpec as P

MESH = pl.DeviceIdType.MESH
S = 0.55
KEEP = (0.0, 0.92, 0.75, 0.45)
TAKE = (0.0, -0.06, -0.18, -0.35)
BF = jnp.bfloat16
Y, X, Z = 0, 1, 2
SPOT = (X, Y, Z)
DIMS = (1, 2, 2, 0, 0, 1)


def table(grades, values):
    out = jnp.zeros(grades.shape, jnp.float32)
    for level in range(1, 4):
        out = jnp.where(grades == level, values[level], out)
    return out


def halves(value):
    high = value.astype(BF)
    low = (value - high.astype(jnp.float32)).astype(BF)
    return high, low


def dot_nt(a, b):
    return lax.dot_general(a, b, (((1,), (1,)), ((), ())), preferred_element_type=jnp.float32)


def dot_nn(a, b):
    return jnp.dot(a, b, preferred_element_type=jnp.float32)


def kernel(
    shape, steps,
    live_ref, e_hbm, h_hbm, me_hbm, mh_hbm, g_hbm, p_hbm, cell_hbm, port_hbm, inj_hbm, wave_hbm,
    eo_hbm, ho_hbm, pw_ref,
    E, H, ME, MH, G, KP, TK, FC, PR, cellT, depthT, curT, rec, J,
    y_low_in, y_high_in, x_low_in, x_high_in, turn_in, cross_in,
    x_low_out, x_high_out, turn_out, cross_out, edge_out, edge, edge_keep, edge_take,
    cell_ref, port_ref, inj_ref, wave_ref,
    part, half, ring, whole,
    load_sem, big_sem, store_sem, send_sem, recv_sem, first_send, first_recv,
    pair_send, pair_recv, ring_send, ring_recv,
):
    nx, ny, nz = shape
    gx, gy = lax.axis_index("gx"), lax.axis_index("gy")
    last_x, last_y = lax.axis_size("gx") - 1, lax.axis_size("gy") - 1
    x_low, x_high = gx > 0, gx < last_x
    y_low, y_high = gy > 0, gy < last_y
    turn_to = jnp.logical_and(x_high, y_low)
    cross_to = jnp.logical_and(x_low, y_high)
    sides = (
        (x_low, (gx - 1, gy)),
        (x_high, (gx + 1, gy)),
        (y_low, (gx, gy - 1)),
        (y_high, (gx, gy + 1)),
        (turn_to, (gx + 1, gy - 1)),
        (cross_to, (gx - 1, gy + 1)),
    )
    core, chip_x, chip_y, chip_z = gx % 2, gx // 2, gy // 4, gy % 4
    partner = (chip_x * 2 + 1 - core, gy)
    places = (chip_x, chip_y, chip_z)

    def fellow(axis, shift):
        if axis == 0:
            return ((chip_x + shift) % 4 * 2 + core, gy)
        if axis == 1:
            return (gx, (chip_y + shift) % 4 * 4 + chip_z)
        return (gx, chip_y * 4 + (chip_z + shift) % 4)

    small = [
        pltpu.make_async_copy(cell_hbm, cell_ref, load_sem.at[0]),
        pltpu.make_async_copy(port_hbm, port_ref, load_sem.at[1]),
        pltpu.make_async_copy(inj_hbm, inj_ref, load_sem.at[2]),
        pltpu.make_async_copy(wave_hbm, wave_ref, load_sem.at[3]),
    ]
    loads = []
    inner = slice(1, ny + 1)
    for x in range(nx):
        pairs = [(e_hbm.at[c, x], E.at[SPOT[c], inner, x]) for c in range(3)]
        pairs += [(h_hbm.at[c, x], H.at[SPOT[c], inner, x]) for c in range(3)]
        pairs += [
            (me_hbm.at[:, x], ME.at[:, inner, x]),
            (g_hbm.at[:, x], G.at[:, inner, x]),
            (mh_hbm.at[:, x], MH.at[:, :, x]),
            (p_hbm.at[x], PR.at[:, x]),
        ]
        loads += [
            pltpu.make_async_copy(source, target, big_sem.at[number, x])
            for number, (source, target) in enumerate(pairs)
        ]
    for copy in loads + small:
        copy.start()

    H[:, 0] = jnp.zeros((3, nx, nz), jnp.float32)
    ME[:, 0] = jnp.zeros((6, nx, nz), jnp.float32)
    G[:, 0] = jnp.zeros((3, nx, nz), jnp.int32)
    for ref in (y_low_in, y_high_in, x_low_in, x_high_in, turn_in, cross_in, edge):
        ref[...] = jnp.zeros_like(ref)
    barrier = pltpu.get_barrier_semaphore()
    for ok, target in sides:
        @pl.when(ok)
        def _():
            pl.semaphore_signal(barrier, inc=1, device_id=target, device_id_type=MESH)

    friends = [partner] + [fellow(axis, shift) for axis in range(3) for shift in range(1, 4)]
    for target in friends:
        pl.semaphore_signal(barrier, inc=1, device_id=target, device_id_type=MESH)

    def remote(source, target_ref, sent, received, target):
        return pltpu.make_async_remote_copy(
            src_ref=source,
            dst_ref=target_ref,
            send_sem=sent,
            recv_sem=received,
            device_id=target,
            device_id_type=MESH,
        )

    def face_copies(slot):
        def one(number, source, target_ref, target):
            return remote(
                source, target_ref.at[slot], send_sem.at[number], recv_sem.at[number, slot], target
            )

        return (
            (y_high, y_low, one(0, E.at[:, ny], y_low_in, (gx, gy + 1))),
            (y_low, y_high, one(1, E.at[1:3, 1], y_high_in, (gx, gy - 1))),
            (turn_to, cross_to, one(2, turn_out, turn_in, (gx + 1, gy - 1))),
            (cross_to, turn_to, one(3, cross_out, cross_in, (gx - 1, gy + 1))),
            (x_high, x_low, one(4, x_high_out, x_low_in, (gx + 1, gy))),
            (x_low, x_high, one(5, x_low_out, x_high_in, (gx - 1, gy))),
        )

    def each(copies, action):
        for sends, receives, copy in copies:
            @pl.when(receives if action == "wait_recv" else sends)
            def _():
                getattr(copy, action)()

    def pack(a):
        at = pl.ds(a, 1)
        for number, c in enumerate((Y, Z)):
            x_low_out[number, at, :] = E[c, a + 1, 0:1, :]
        for c in range(3):
            x_high_out[c, at, :] = E[c, a + 1, nx - 1 : nx, :]

    def pack_corners():
        turn_out[...] = E[X, 1, nx - 1 : nx, :]
        cross_out[...] = E[Y, ny, 0:1, :]

    for copy in loads:
        copy.wait()

    @pl.loop(0, ny)
    def _(a):
        pack(a)
        at, end = pl.ds(a, 1), slice(nx - 1, nx)
        edge_out[0, at, :] = H[Y, a + 1, end, :]
        edge_out[1, at, :] = H[Z, a + 1, end, :]
        for k in range(4):
            edge_out[2 + k, at, :] = ME[2 + k, a + 1, end, :]
        for d in range(3):
            edge_out[6 + d, at, :] = G[d, a + 1, end, :].astype(jnp.float32)

    pack_corners()
    pl.semaphore_wait(barrier, sum(ok.astype(jnp.int32) for ok, _ in sides) + len(friends))
    up = (gx, gy + 1)
    firsts = [
        (x_high, x_low, edge_out, edge, (gx + 1, gy)),
        (y_high, y_low, G.at[:, ny], G.at[:, 0], up),
        (y_high, y_low, H.at[1:3, ny], H.at[1:3, 0], up),
        (y_high, y_low, ME.at[0:2, ny], ME.at[0:2, 0], up),
        (y_high, y_low, ME.at[4:6, ny], ME.at[4:6, 0], up),
    ]
    firsts = [
        (sends, receives, remote(source, target_ref, first_send.at[i], first_recv.at[i], target))
        for i, (sends, receives, source, target_ref, target) in enumerate(firsts)
    ]
    each(firsts, "start")
    each(face_copies(0), "start")

    for copy in small:
        copy.wait()
    slots = cell_ref.shape[1]
    cell = (cell_ref[1:2, :] - gy * ny) * nx + (cell_ref[0:1, :] - gx * nx)
    cellT[...] = (
        lax.broadcasted_iota(jnp.int32, (nx * ny, slots), 0) == cell
    ).astype(jnp.float32)
    depthT[...] = (
        lax.broadcasted_iota(jnp.int32, (nz, slots), 0) == cell_ref[2:3, :]
    ).astype(jnp.float32).astype(BF)
    live = lax.broadcasted_iota(jnp.int32, (1, slots), 1) < live_ref[0]
    curT[...] = jnp.where(live, dot_nt(wave_ref[...], inj_ref[...]), 0.0)

    @pl.loop(0, ny)
    def _(a):
        for d in range(3):
            grades = G[d, a + 1]
            KP[d, a + 1] = table(grades, KEEP)
            TK[d, a + 1] = table(grades, TAKE)
        FC[a] = S / PR[a]

    each(firsts, "wait_recv")
    each(firsts, "wait_send")
    for d in range(3):
        KP[d, 0] = table(G[d, 0], KEEP)
        TK[d, 0] = table(G[d, 0], TAKE)
        edge_keep[d] = table(edge[6 + d], KEEP)
        edge_take[d] = table(edge[6 + d], TAKE)

    row = lax.broadcasted_iota(jnp.int32, (nx, nz), 0)
    lane = lax.broadcasted_iota(jnp.int32, (nx, nz), 1)
    x_scale = jnp.where(x_low, S, 0.0)
    y_scale = jnp.where(y_low, S, 0.0)

    def next_row(v, fill):
        return jnp.where(row == nx - 1, fill, pltpu.roll(v, nx - 1, 0))

    def prev_row(v, fill):
        return jnp.where(row == 0, fill, pltpu.roll(v, 1, 0))

    def next_z(v):
        return jnp.where(lane == nz - 1, 0.0, pltpu.roll(v, nz - 1, 1))

    def prev_z(v):
        return jnp.where(lane == 0, 0.0, pltpu.roll(v, 1, 1))

    def term(k, slope, memory, a, shift):
        d = DIMS[k]
        carried = KP[d, a + 1] * memory[k, a + shift] + TK[d, a + 1] * slope
        memory[k, a + shift] = carried
        return slope + carried

    def h_plane(a, slot, above_x, above_z):
        ex, ey, ez = E[X, a + 1], E[Y, a + 1], E[Z, a + 1]
        at = pl.ds(a, 1)
        slopes = (
            above_z - ez,
            next_z(ey) - ey,
            next_z(ex) - ex,
            next_row(ez, x_high_in[slot, 1, at, :]) - ez,
            next_row(ey, x_high_in[slot, 0, at, :]) - ey,
            above_x - ex,
        )
        t = [term(k, slope, ME, a, 1) for k, slope in enumerate(slopes)]
        for c in range(3):
            spot = SPOT[c]
            H[spot, a + 1] = H[spot, a + 1] - S * (t[2 * c] - t[2 * c + 1])

    def h_below(slot):
        ey, ex, ez = (y_low_in[slot, c] for c in range(3))
        t0 = term(0, E[Z, 1] - ez, ME, -1, 1)
        t1 = term(1, next_z(ey) - ey, ME, -1, 1)
        t4 = term(4, next_row(ey, cross_in_row(slot)) - ey, ME, -1, 1)
        t5 = term(5, E[X, 1] - ex, ME, -1, 1)
        H[X, 0] = H[X, 0] - y_scale * (t0 - t1)
        H[Z, 0] = H[Z, 0] - y_scale * (t4 - t5)

    def cross_in_row(slot):
        return cross_in[slot]

    def h_edge(slot):
        ey, ex, ez = (x_low_in[slot, c] for c in range(3))
        slopes = (
            next_z(ex) - ex,
            x_low_out[1] - ez,
            x_low_out[0] - ey,
            next_row(ex, 0.0) - ex,
        )
        t = []
        for k, slope in enumerate(slopes):
            d = DIMS[2 + k]
            carried = edge_keep[d] * edge[2 + k] + edge_take[d] * slope
            edge[2 + k] = carried
            t.append(slope + carried)
        edge[0] = edge[0] - x_scale * (t[0] - t[1])
        edge[1] = edge[1] - x_scale * (t[2] - t[3])

    def h_edge_end(slot):
        end = slice(ny - 1, ny)
        corner = turn_in[slot]
        moved = edge_take[1, end, :] * corner
        edge[5, end, :] = edge[5, end, :] + moved
        edge[1, end, :] = edge[1, end, :] + x_scale * (corner + moved)

    def e_plane(a):
        hx, hy, hz = H[X, a + 1], H[Y, a + 1], H[Z, a + 1]
        at = pl.ds(a, 1)
        slopes = (
            hz - H[Z, a],
            hy - prev_z(hy),
            hx - prev_z(hx),
            hz - prev_row(hz, edge[1, at, :]),
            hy - prev_row(hy, edge[0, at, :]),
            hx - H[X, a],
        )
        t = [term(k, slope, MH, a, 0) for k, slope in enumerate(slopes)]
        factor = FC[a]
        E[X, a + 1] = E[X, a + 1] + factor * (t[0] - t[1])
        E[Y, a + 1] = E[Y, a + 1] + factor * (t[2] - t[3])
        source = J[pl.ds(a * nx, nx), :]
        E[Z, a + 1] = E[Z, a + 1] + factor * (t[4] - t[5]) - source

    def drive(t):
        high, low = halves(E[Z, 1 : ny + 1].reshape(nx * ny, nz))
        picked = dot_nn(high, depthT[...]) + dot_nn(low, depthT[...])
        value = jnp.sum(picked * cellT[...], axis=0, keepdims=True)
        rec[pl.ds(t, 1), :] = value * curT[pl.ds(t, 1), :]

    def sources(t):
        high, low = halves(S * curT[pl.ds(t, 1), :])
        mask = cellT[...].astype(BF)
        J[...] = dot_nt(mask * high, depthT[...]) + dot_nt(mask * low, depthT[...])

    @pl.loop(0, steps)
    def _(t):
        slot = t % 2
        copies = face_copies(slot)

        @pl.when(t > 0)
        def _():
            drive(t - 1)

        sources(t)
        each(copies[4:], "wait_recv")
        each(copies[4:], "wait_send")
        h_edge(slot)

        @pl.loop(0, ny - 1)
        def _(a):
            h_plane(a, slot, E[X, a + 2], E[Z, a + 2])

        @pl.loop(1, ny - 1)
        def _(a):
            e_plane(a)
            pack(a)

        each(copies[:4], "wait_recv")
        each(copies[:4], "wait_send")
        h_below(slot)
        h_plane(ny - 1, slot, y_high_in[slot, 0], y_high_in[slot, 1])
        h_edge_end(slot)
        e_plane(0)
        e_plane(ny - 1)
        pack_corners()
        pack(0)
        pack(ny - 1)

        @pl.when(t < steps - 1)
        def _():
            each(face_copies(1 - slot), "start")

    stores = [
        pltpu.make_async_copy(field.at[SPOT[c], inner, x], out.at[c, x], store_sem.at[i, c, x])
        for i, (field, out) in enumerate(((E, eo_hbm), (H, ho_hbm)))
        for c in range(3)
        for x in range(nx)
    ]
    for copy in stores:
        copy.start()
    drive(steps - 1)
    rows, ports = half.shape
    members = (
        lax.broadcasted_iota(jnp.int32, (ports, slots), 0) == port_ref[...]
    ).astype(jnp.float32).astype(BF)
    high, low = halves(rec[...])
    total = dot_nt(high, members) + dot_nt(low, members)
    part[0] = total[0:rows]
    part[1] = total[rows : 2 * rows]

    def swap(number, source, target_ref):
        return pltpu.make_async_remote_copy(
            src_ref=source,
            dst_ref=target_ref,
            send_sem=pair_send.at[number],
            recv_sem=pair_recv.at[number],
            device_id=partner,
            device_id_type=MESH,
        )

    def send(axis, shift):
        return pltpu.make_async_remote_copy(
            src_ref=ring.at[axis, places[axis]],
            dst_ref=ring.at[axis, places[axis]],
            send_sem=ring_send.at[axis, shift],
            recv_sem=ring_recv.at[axis, shift],
            device_id=fellow(axis, shift),
            device_id_type=MESH,
        )

    def arrival(axis, shift):
        slot = (places[axis] + 4 - shift) % 4
        return pltpu.make_async_remote_copy(
            src_ref=ring.at[axis, slot],
            dst_ref=ring.at[axis, slot],
            send_sem=ring_send.at[axis, shift],
            recv_sem=ring_recv.at[axis, shift],
            device_id=fellow(axis, shift),
            device_id_type=MESH,
        )

    trade = swap(0, part.at[1 - core], half)
    trade.start()
    trade.wait()
    value = part[core] + half[...]
    for axis in range(3):
        ring[axis, places[axis]] = value
        for shift in range(1, 4):
            send(axis, shift).start()
        for shift in range(1, 4):
            arrival(axis, shift).wait_recv()
        value = (ring[axis, 0] + ring[axis, 1]) + (ring[axis, 2] + ring[axis, 3])
    whole[core] = value
    trade = swap(1, whole.at[core], whole.at[core])
    trade.start()
    for axis in range(3):
        for shift in range(1, 4):
            send(axis, shift).wait_send()
    trade.wait()
    pw_ref[0:rows] = whole[0]
    pw_ref[rows : 2 * rows] = whole[1]
    for copy in stores:
        copy.wait()


def local(
    electric, magnetic, aux_electric, aux_magnetic, grades, permittivity,
    dipole_cell, dipole_port, live_count, injection, waveform,
):
    shape = electric.shape[1:]
    nx, ny, nz = shape
    slots = dipole_cell.shape[1]
    ports, steps = waveform.shape
    f32 = jnp.float32
    anywhere = pl.BlockSpec(memory_space=pl.ANY)
    vmem = pl.BlockSpec(memory_space=pltpu.VMEM)
    half = (steps // 2, ports)
    return pl.pallas_call(
        functools.partial(kernel, shape, steps),
        out_shape=(
            jax.ShapeDtypeStruct(electric.shape, f32),
            jax.ShapeDtypeStruct(magnetic.shape, f32),
            jax.ShapeDtypeStruct((steps, ports), f32),
        ),
        in_specs=[pl.BlockSpec(memory_space=pltpu.SMEM)] + [anywhere] * 10,
        out_specs=(anywhere, anywhere, vmem),
        scratch_shapes=[
            pltpu.VMEM((3, ny + 1, nx, nz), f32),
            pltpu.VMEM((3, ny + 1, nx, nz), f32),
            pltpu.VMEM((6, ny + 1, nx, nz), f32),
            pltpu.VMEM((6, ny, nx, nz), f32),
            pltpu.VMEM((3, ny + 1, nx, nz), jnp.int32),
            pltpu.VMEM((3, ny + 1, nx, nz), f32),
            pltpu.VMEM((3, ny + 1, nx, nz), f32),
            pltpu.VMEM((ny, nx, nz), f32),
            pltpu.VMEM((ny, nx, nz), f32),
            pltpu.VMEM((nx * ny, slots), f32),
            pltpu.VMEM((nz, slots), BF),
            pltpu.VMEM((steps, slots), f32),
            pltpu.VMEM((steps, slots), f32),
            pltpu.VMEM((nx * ny, nz), f32),
            pltpu.VMEM((2, 3, nx, nz), f32),
            pltpu.VMEM((2, 2, nx, nz), f32),
            pltpu.VMEM((2, 3, ny, nz), f32),
            pltpu.VMEM((2, 2, ny, nz), f32),
            pltpu.VMEM((2, 1, nz), f32),
            pltpu.VMEM((2, 1, nz), f32),
            pltpu.VMEM((2, ny, nz), f32),
            pltpu.VMEM((3, ny, nz), f32),
            pltpu.VMEM((1, nz), f32),
            pltpu.VMEM((1, nz), f32),
            pltpu.VMEM((9, ny, nz), f32),
            pltpu.VMEM((9, ny, nz), f32),
            pltpu.VMEM((3, ny, nz), f32),
            pltpu.VMEM((3, ny, nz), f32),
            pltpu.VMEM((3, slots), jnp.int32),
            pltpu.VMEM((1, slots), jnp.int32),
            pltpu.VMEM((slots, ports), BF),
            pltpu.VMEM((steps, ports), BF),
            pltpu.VMEM((2,) + half, f32),
            pltpu.VMEM(half, f32),
            pltpu.VMEM((3, 4) + half, f32),
            pltpu.VMEM((2,) + half, f32),
            pltpu.SemaphoreType.DMA((4,)),
            pltpu.SemaphoreType.DMA((10, nx)),
            pltpu.SemaphoreType.DMA((2, 3, nx)),
            pltpu.SemaphoreType.DMA((6,)),
            pltpu.SemaphoreType.DMA((6, 2)),
            pltpu.SemaphoreType.DMA((5,)),
            pltpu.SemaphoreType.DMA((5,)),
            pltpu.SemaphoreType.DMA((2,)),
            pltpu.SemaphoreType.DMA((2,)),
            pltpu.SemaphoreType.DMA((3, 4)),
            pltpu.SemaphoreType.DMA((3, 4)),
        ],
        compiler_params=pltpu.CompilerParams(
            collective_id=0, has_side_effects=True, vmem_limit_bytes=67_043_328
        ),
    )(
        live_count, electric, magnetic, aux_electric, aux_magnetic, grades, permittivity,
        dipole_cell, dipole_port.reshape(1, slots), injection, waveform.T,
    )


def solution(mesh):
    block = P(None, "gx", "gy", None)
    each = ("gx", "gy")
    return jax.shard_map(
        local,
        mesh=mesh,
        in_specs=(
            block, block, block, block, block, P("gx", "gy", None),
            P(None, each), P(each), P(each), P(each, None), P(),
        ),
        out_specs=(block, block, P()),
        check_vma=False,
    )
```

time: 159 us -> 124 us (0.78)
  Pallas kernels: 154 us -> 119 us
    pallas_call x1, Pallas kernels: 154 us -> 119 us  [local(): pl.pallas_call(functools.partial(kernel, shape, steps), out_shape=(jax.Sh...]
where the time goes in v3:
time: 124 us
  Pallas kernels  119 us (96%)
  local copies, waits for them, and re-layouts  3.64 us (3%)
  between operations  1.31 us (1%)
    pallas_call x1, Pallas kernels, local(): pl.pallas_call(functools.partial(kernel, shape, steps), out_shape=(jax.Sh...  119 us
    unnamed x7, local copies, waits for them, and re-layouts  3.64 us

profile of v3, /device:TPU:1, one launch (start us, length us, event | category | flops | bytes accessed | tf_op | source)
XLA Modules:
  0.0 124.0 jit_solution(7307831337293302972)
XLA Ops:
  1.3 119.0 %shard_map.130 = (f32[3,16,16,256]{3,2,1,0:T(8,128)}, f32[3,16,16,256]{3,2,1,0:T(8,128)}, f32[16,512]{1,0:T(8,128)}) custom-call(s32[1]{0:T(128)S(6)} %copy.17.live_ref, f32[3,16,16,256]{3,2,1,0:T(8,128)} %e_hbm.1, f32[3,16,16,256]{3,2,1,0:T(8,128)} %h_hbm.1, f32[6,16,16,256]{3,2,1,0:T(8,128)} %me_hbm.1, f32[6,16,16,256]{3,2,1,0:T(8,128)} %mh_hbm.1, ...), custom_call_target="tpu_custom_call" | custom-call | tf_op jit(solution)/shard_map/pallas_call | solution.py:447
  120.3 0.0 copy-start
  120.3 0.0 copy-start.1
  120.3 2.1 %copy.18 = f32[3,16,16,256]{3,2,1,0:T(8,128)} copy(f32[3,16,16,256]{3,2,1,0:T(8,128)} %get-tuple-element.6) | data formatting | bytes 1572864
  122.5 0.0 copy-done
  122.5 0.9 copy.19
  123.3 0.0 copy-done.1
  123.3 0.6 copy.20
Async XLA Ops:
  120.3 2.2 %copy-start = (f32[3,16,16,256]{3,2,1,0:T(8,128)S(1)}, f32[3,16,16,256]{3,2,1,0:T(8,128)}, u32[]{:S(2)}) copy-start(f32[3,16,16,256]{3,2,1,0:T(8,128)} %get-tuple-element.7) | copy-start | bytes 2359300
  120.3 3.0 %copy-start.1 = (f32[16,512]{1,0:T(8,128)S(1)}, f32[16,512]{1,0:T(8,128)}, u32[]{:S(2)}) copy-start(f32[16,512]{1,0:T(8,128)} %get-tuple-element.8) | copy-start | bytes 98308

commit v4 on v3

--- a/solution.py
+++ b/solution.py
@@ -82,22 +82,25 @@
         pltpu.make_async_copy(inj_hbm, inj_ref, load_sem.at[2]),
         pltpu.make_async_copy(wave_hbm, wave_ref, load_sem.at[3]),
     ]
-    loads = []
     inner = slice(1, ny + 1)
-    for x in range(nx):
-        pairs = [(e_hbm.at[c, x], E.at[SPOT[c], inner, x]) for c in range(3)]
-        pairs += [(h_hbm.at[c, x], H.at[SPOT[c], inner, x]) for c in range(3)]
+
+    def plane_loads(a):
+        pairs = [(e_hbm.at[c, :, a], E.at[SPOT[c], a + 1]) for c in range(3)]
+        pairs += [(h_hbm.at[c, :, a], H.at[SPOT[c], a + 1]) for c in range(3)]
         pairs += [
-            (me_hbm.at[:, x], ME.at[:, inner, x]),
-            (g_hbm.at[:, x], G.at[:, inner, x]),
-            (mh_hbm.at[:, x], MH.at[:, :, x]),
-            (p_hbm.at[x], PR.at[:, x]),
+            (me_hbm.at[:, :, a], ME.at[:, a + 1]),
+            (g_hbm.at[:, :, a], G.at[:, a + 1]),
+            (mh_hbm.at[:, :, a], MH.at[:, a]),
+            (p_hbm.at[:, a], PR.at[a]),
         ]
-        loads += [
-            pltpu.make_async_copy(source, target, big_sem.at[number, x])
+        return [
+            pltpu.make_async_copy(source, target, big_sem.at[number, a])
             for number, (source, target) in enumerate(pairs)
         ]
-    for copy in loads + small:
+
+    top = plane_loads(ny - 1)
+    loads = [copy for a in range(ny - 1) for copy in plane_loads(a)]
+    for copy in top + loads + small:
         copy.start()
 
     H[:, 0] = jnp.zeros((3, nx, nz), jnp.float32)
@@ -157,22 +160,6 @@
         turn_out[...] = E[X, 1, nx - 1 : nx, :]
         cross_out[...] = E[Y, ny, 0:1, :]
 
-    for copy in loads:
-        copy.wait()
-
-    @pl.loop(0, ny)
-    def _(a):
-        pack(a)
-        at, end = pl.ds(a, 1), slice(nx - 1, nx)
-        edge_out[0, at, :] = H[Y, a + 1, end, :]
-        edge_out[1, at, :] = H[Z, a + 1, end, :]
-        for k in range(4):
-            edge_out[2 + k, at, :] = ME[2 + k, a + 1, end, :]
-        for d in range(3):
-            edge_out[6 + d, at, :] = G[d, a + 1, end, :].astype(jnp.float32)
-
-    pack_corners()
-    pl.semaphore_wait(barrier, sum(ok.astype(jnp.int32) for ok, _ in sides) + len(friends))
     up = (gx, gy + 1)
     firsts = [
         (x_high, x_low, edge_out, edge, (gx + 1, gy)),
@@ -185,8 +172,28 @@
         (sends, receives, remote(source, target_ref, first_send.at[i], first_recv.at[i], target))
         for i, (sends, receives, source, target_ref, target) in enumerate(firsts)
     ]
-    each(firsts, "start")
-    each(face_copies(0), "start")
+    for copy in top:
+        copy.wait()
+    pl.semaphore_wait(barrier, sum(ok.astype(jnp.int32) for ok, _ in sides) + len(friends))
+    each(face_copies(0)[:1], "start")
+    each(firsts[1:], "start")
+    for copy in loads:
+        copy.wait()
+
+    @pl.loop(0, ny)
+    def _(a):
+        pack(a)
+        at, end = pl.ds(a, 1), slice(nx - 1, nx)
+        edge_out[0, at, :] = H[Y, a + 1, end, :]
+        edge_out[1, at, :] = H[Z, a + 1, end, :]
+        for k in range(4):
+            edge_out[2 + k, at, :] = ME[2 + k, a + 1, end, :]
+        for d in range(3):
+            edge_out[6 + d, at, :] = G[d, a + 1, end, :].astype(jnp.float32)
+
+    pack_corners()
+    each(face_copies(0)[1:], "start")
+    each(firsts[:1], "start")
 
     for copy in small:
         copy.wait()
@@ -209,14 +216,6 @@
             TK[d, a + 1] = table(grades, TAKE)
         FC[a] = S / PR[a]
 
-    each(firsts, "wait_recv")
-    each(firsts, "wait_send")
-    for d in range(3):
-        KP[d, 0] = table(G[d, 0], KEEP)
-        TK[d, 0] = table(G[d, 0], TAKE)
-        edge_keep[d] = table(edge[6 + d], KEEP)
-        edge_take[d] = table(edge[6 + d], TAKE)
-
     row = lax.broadcasted_iota(jnp.int32, (nx, nz), 0)
     lane = lax.broadcasted_iota(jnp.int32, (nx, nz), 1)
     x_scale = jnp.where(x_low, S, 0.0)
@@ -333,31 +332,58 @@
         sources(t)
         each(copies[4:], "wait_recv")
         each(copies[4:], "wait_send")
+
+        @pl.when(t == 0)
+        def _():
+            each(firsts[:1], "wait_recv")
+            each(firsts[:1], "wait_send")
+            for d in range(3):
+                edge_keep[d] = table(edge[6 + d], KEEP)
+                edge_take[d] = table(edge[6 + d], TAKE)
+
         h_edge(slot)
 
-        @pl.loop(0, ny - 1)
-        def _(a):
-            h_plane(a, slot, E[X, a + 2], E[Z, a + 2])
-
-        @pl.loop(1, ny - 1)
-        def _(a):
-            e_plane(a)
-            pack(a)
+        @pl.loop(0, 3)
+        def _(g):
+            for i in range(5):
+                a = g * 5 + i
+                h_plane(a, slot, E[X, a + 2], E[Z, a + 2])
+
+        @pl.loop(0, 2)
+        def _(g):
+            for i in range(7):
+                a = g * 7 + 1 + i
+                e_plane(a)
+                pack(a)
 
         each(copies[:4], "wait_recv")
         each(copies[:4], "wait_send")
+
+        @pl.when(t == 0)
+        def _():
+            each(firsts[1:], "wait_recv")
+            each(firsts[1:], "wait_send")
+            for d in range(3):
+                KP[d, 0] = table(G[d, 0], KEEP)
+                TK[d, 0] = table(G[d, 0], TAKE)
+
         h_below(slot)
         h_plane(ny - 1, slot, y_high_in[slot, 0], y_high_in[slot, 1])
         h_edge_end(slot)
         e_plane(0)
         e_plane(ny - 1)
         pack_corners()
+
+        @pl.when(t < steps - 1)
+        def _():
+            each(face_copies(1 - slot)[:4], "start")
+
         pack(0)
         pack(ny - 1)
 
         @pl.when(t < steps - 1)
         def _():
-            each(face_copies(1 - slot), "start")
+            each(face_copies(1 - slot)[4:], "start")
 
     stores = [
         pltpu.make_async_copy(field.at[SPOT[c], inner, x], out.at[c, x], store_sem.at[i, c, x])
@@ -442,6 +468,7 @@
     ports, steps = waveform.shape
     f32 = jnp.float32
     anywhere = pl.BlockSpec(memory_space=pl.ANY)
+    hbm = pl.BlockSpec(memory_space=pltpu.HBM)
     vmem = pl.BlockSpec(memory_space=pltpu.VMEM)
     half = (steps // 2, ports)
     return pl.pallas_call(
@@ -451,7 +478,7 @@
             jax.ShapeDtypeStruct(magnetic.shape, f32),
             jax.ShapeDtypeStruct((steps, ports), f32),
         ),
-        in_specs=[pl.BlockSpec(memory_space=pltpu.SMEM)] + [anywhere] * 10,
+        in_specs=[pl.BlockSpec(memory_space=pltpu.SMEM)] + [hbm] * 10,
         out_specs=(anywhere, anywhere, vmem),
         scratch_shapes=[
             pltpu.VMEM((3, ny + 1, nx, nz), f32),
@@ -491,7 +518,7 @@
             pltpu.VMEM((3, 4) + half, f32),
             pltpu.VMEM((2,) + half, f32),
             pltpu.SemaphoreType.DMA((4,)),
-            pltpu.SemaphoreType.DMA((10, nx)),
+            pltpu.SemaphoreType.DMA((10, ny)),
             pltpu.SemaphoreType.DMA((2, 3, nx)),
             pltpu.SemaphoreType.DMA((6,)),
             pltpu.SemaphoreType.DMA((6, 2)),

time: 124 us -> 102 us (0.82)
  Pallas kernels: 119 us -> 96.9 us
    pallas_call x1, Pallas kernels: 119 us -> 96.9 us  [local(): pl.pallas_call(functools.partial(kernel, shape, steps), out_shape=(jax.Sh...]
where the time goes in v4:
time: 102 us
  Pallas kernels  96.9 us (95%)
  local copies, waits for them, and re-layouts  3.64 us (4%)
  between operations  1.31 us (1%)
    pallas_call x1, Pallas kernels, local(): pl.pallas_call(functools.partial(kernel, shape, steps), out_shape=(jax.Sh...  96.9 us
    unnamed x7, local copies, waits for them, and re-layouts  3.64 us

profile of v4, /device:TPU:1, one launch (start us, length us, event | category | flops | bytes accessed | tf_op | source)
XLA Modules:
  0.0 101.8 jit_solution(2593137979270161618)
XLA Ops:
  1.3 96.9 %shard_map.130 = (f32[3,16,16,256]{3,2,1,0:T(8,128)}, f32[3,16,16,256]{3,2,1,0:T(8,128)}, f32[16,512]{1,0:T(8,128)}) custom-call(s32[1]{0:T(128)S(6)} %copy.17.live_ref, f32[3,16,16,256]{3,2,1,0:T(8,128)} %e_hbm.1, f32[3,16,16,256]{3,2,1,0:T(8,128)} %h_hbm.1, f32[6,16,16,256]{3,2,1,0:T(8,128)} %me_hbm.1, f32[6,16,16,256]{3,2,1,0:T(8,128)} %mh_hbm.1, ...), custom_call_target="tpu_custom_call" | custom-call | tf_op jit(solution)/shard_map/pallas_call | solution.py:474
  98.2 0.0 copy-start
  98.2 0.0 copy-start.1
  98.2 2.1 %copy.18 = f32[3,16,16,256]{3,2,1,0:T(8,128)} copy(f32[3,16,16,256]{3,2,1,0:T(8,128)} %get-tuple-element.6) | data formatting | bytes 1572864
  100.3 0.0 copy-done
  100.3 0.9 copy.19
  101.2 0.0 copy-done.1
  101.2 0.6 copy.20
Async XLA Ops:
  98.2 2.2 %copy-start = (f32[3,16,16,256]{3,2,1,0:T(8,128)S(1)}, f32[3,16,16,256]{3,2,1,0:T(8,128)}, u32[]{:S(2)}) copy-start(f32[3,16,16,256]{3,2,1,0:T(8,128)} %get-tuple-element.7) | copy-start | bytes 2359300
  98.2 3.0 %copy-start.1 = (f32[16,512]{1,0:T(8,128)S(1)}, f32[16,512]{1,0:T(8,128)}, u32[]{:S(2)}) copy-start(f32[16,512]{1,0:T(8,128)} %get-tuple-element.8) | copy-start | bytes 98308
